TPU v7x, 256 devices: a whole 4x4x8 slice. The times are simulated.
256 devices in a mesh: band: 8 (over z_lo, core), lane: 32 (over z_hi, y, x).
Axes of the slice: x: 4, y: 4, z: 8 (z_hi: 2, z_lo: 4; z = z_hi * 4 + z_lo), core: 2. Of those that a mesh axis runs over, the one named last changes fastest.
Arguments:
- load_terms: float32 [512, 2048, 128], P('band', 'lane'), may hold values from -6 to 6
- start_values: float32 [512, 2048, 128], P('band', 'lane'), may hold values from -6 to 6
- reaction_rate: float32 [512, 2048, 128], P('band', 'lane'), may hold values from 0.1 to 0.9
Outputs:
- solution: float32 [512, 2048, 128], P('band', 'lane')
All inputs are finite; a program needn't handle non-finite values.
Results may differ from a plain program's by a relative error of at most 0.0003.
Values sent between devices are 32-bit elements.
No kernel may reach another device: no remote copies, remote signals or barrier semaphores. Data moves between devices by JAX's collectives and lax.ppermute only.
A program may use at most 64 MiB of HBM per device.

v0:
```python
import jax
import jax.numpy as jnp
from jax import lax
from jax.experimental import pallas as pl
from jax.experimental.pallas import tpu as pltpu
from jax.sharding import PartitionSpec as P

RATIO = 4
BEFORE = 3
AFTER = 2
INNER = 13

N = 64
C = N // RATIO
L = 128
DS = BEFORE + 1
DF = DS - 1
DEPTH = DS + 2 * DF
AT_LOAD, AT_MASS = N * DS, N * (DS + DF)
FINE = N * DEPTH
R0, C0 = DS, 12
R1, C1 = R0 + N, C0 + N
ROWS, COLS = R1 + DS, C1 + 12
LEFT, RIGHT = slice(C0 - 4, C0 + 4), slice(C1 - 4, C1 + 4)
FULL = ((C0 - 4, C0 + 20), (C0 + 20, C0 + 44), (C0 + 44, C0 + 68))
EDGES = ((C0 - 4, C0 + 4), (C1 - 4, C1 + 4))
H = INNER
CR0, CC0 = H, 20
CR, CCOLS = C + 2 * H, 56
WIDTHS = [C + 2 * (H + 1 - j) for j in range(1, H + 1)]
STARTS = [sum(WIDTHS[:k]) for k in range(H)]
BAND_COARSE = -(-sum(WIDTHS) // 8) * 8
BAND_RIM = N + 8
LANE_COARSE = C * H
FIT = 16 * 2**20

f32 = jnp.float32


def parity(axis):
    return lax.rem(lax.axis_index(axis), 2) == 0


def either(test, one, other):
    @pl.when(test)
    def _():
        one()

    @pl.when(jnp.logical_not(test))
    def _():
        other()


def sds(*shape):
    return jax.ShapeDtypeStruct(shape, f32)


VM = pl.BlockSpec(memory_space=pltpu.VMEM)
HBM = pl.BlockSpec(memory_space=pltpu.HBM)


def call(body, outs, ins, scratch=(), aliases=None, flops=10**6, name=None, inner=True):
    return pl.pallas_call(
        body,
        out_shape=[pltpu.VMEM(o.shape, o.dtype) for o in outs] if inner else outs,
        in_specs=ins,
        out_specs=[VM] * len(outs),
        scratch_shapes=list(scratch),
        input_output_aliases=aliases or {},
        compiler_params=pltpu.CompilerParams(vmem_limit_bytes=FIT),
        cost_estimate=pl.CostEstimate(flops=flops, bytes_accessed=8 * 10**6, transcendentals=0),
        name=name,
    )


def loop(count, per, body):
    def turn(g, carry):
        for k in range(per):
            body(g * per + k)
        return carry

    lax.fori_loop(0, count // per, turn, 0)


def gather_columns(line, row):
    line[...] = row
    total = line[pl.ds(0, C, stride=RATIO), :]
    for k in range(1, RATIO):
        total = total + line[pl.ds(k, C, stride=RATIO), :]
    return total * (1.0 / RATIO)


def pack_fine(load, start, mass_hbm, m_even, m_odd, b_even, b_odd, mass, cm, side, line, sem_side, sem_mass, sem_band):
    whole = pltpu.make_async_copy(mass_hbm, mass, sem_mass.at[0])
    copies = []
    for k, src in enumerate((start, load)):
        for s, at in enumerate((0, N - 8)):
            copies.append(
                pltpu.make_async_copy(src.at[:, pl.ds(at, 8)], side.at[k, s], sem_side.at[k, s])
            )
    even = parity("band")
    bands = []
    for which, (dst, bottom) in enumerate(((b_even, even), (b_odd, jnp.logical_not(even)))):
        at = 0
        for k, (src, depth) in enumerate(((start, DS), (load, DF), (mass_hbm, DF))):
            first = jnp.where(bottom, N - depth, 0)
            bands.append(
                pltpu.make_async_copy(
                    src.at[pl.ds(first, depth)], dst.at[pl.ds(at, depth)], sem_band.at[which, k]
                )
            )
            at += depth
    for c in copies:
        c.start()
    whole.start()
    for c in bands:
        c.start()
    for c in copies:
        c.wait()

    def pack(right, left):
        def group(g, carry):
            for k, (depth, field) in enumerate(((DS, 0), (DF, AT_LOAD))):
                base = pl.multiple_of(g * (8 * depth), 8)
                for r in range(8):
                    at = field + base + r * depth
                    right[pl.ds(at, depth), :] = side[k, 1, g * 8 + r, 8 - depth :, :]
                    left[pl.ds(at, depth), :] = side[k, 0, g * 8 + r, :depth, :]
            return carry

        lax.fori_loop(0, N // 8, group, 0)

    lane_even = parity("lane")
    either(lane_even, lambda: pack(m_even, m_odd), lambda: pack(m_odd, m_even))
    whole.wait()

    def pack_mass(right, left):
        def group(g, carry):
            base = pl.multiple_of(g * (8 * DF), 8)
            for half in range(2):
                total = None
                for k in range(RATIO):
                    r = half * RATIO + k
                    at = AT_MASS + base + r * DF
                    row = mass[g * 8 + r]
                    total = row if total is None else total + row
                    right[pl.ds(at, DF), :] = row[N - DF :, :]
                    left[pl.ds(at, DF), :] = row[:DF, :]
                cm[2 * g + half] = gather_columns(line.at[half], total)
            return carry

        lax.fori_loop(0, N // 8, group, 0)
        pack_coarse_lanes(cm, right, left, FINE)

    either(lane_even, lambda: pack_mass(m_even, m_odd), lambda: pack_mass(m_odd, m_even))
    for c in bands:
        c.wait()


def pack_corners(m_even, m_odd, token, c_even, c_odd):
    del token

    def fill(left, right):
        def put(dst, bottom):
            at = 0
            for src in (left, right):
                for field, depth in ((0, DS), (AT_LOAD, DF), (AT_MASS, DF)):
                    lo, size = field + (N - DF) * depth * bottom, DF * depth
                    dst[at : at + size, :] = src[lo : lo + size, :]
                    at += size

        either(
            parity("band"),
            lambda: (put(c_even, 1), put(c_odd, 0)),
            lambda: (put(c_even, 0), put(c_odd, 1)),
        )

    either(parity("lane"), lambda: fill(m_odd, m_even), lambda: fill(m_even, m_odd))


def pack_coarse_lanes(own, right, left, at):
    for i in range(C):
        lo = at + i * H
        row = own[i]
        right[lo : lo + H, :] = row[C - H :, :]
        left[lo : lo + H, :] = row[:H, :]


def place_coarse_lanes(ext, left, right, at):
    for i in range(C):
        lo = at + i * H
        ext[CR0 + i, CC0 - H : CC0, :] = left[lo : lo + H, :]
        ext[CR0 + i, CC0 + C : CC0 + C + H, :] = right[lo : lo + H, :]


def pack_coarse_bands(ext, down, up):
    for j in range(1, H + 1):
        reach, at, wide = H + 1 - j, STARTS[j - 1], WIDTHS[j - 1]
        cols = slice(CC0 - reach, CC0 + C + reach)
        down[at : at + wide, :] = ext[CR0 + C - j, cols, :]
        up[at : at + wide, :] = ext[CR0 + j - 1, cols, :]
    for dst in (down, up):
        dst[sum(WIDTHS) : BAND_COARSE, :] = jnp.zeros((BAND_COARSE - sum(WIDTHS), L), f32)


def place_coarse_bands(ext, above, below):
    for j in range(1, H + 1):
        reach, at, wide = H + 1 - j, STARTS[j - 1], WIDTHS[j - 1]
        cols = slice(CC0 - reach, CC0 + C + reach)
        ext[CR0 - j, cols, :] = above[at : at + wide, :]
        ext[CR0 + C + j - 1, cols, :] = below[at : at + wide, :]


def weight(mass):
    return 0.8 / (4.0 + mass)


def sweep_rows(src, dst, w, f, first, last, segments, per=4):
    def some(r, count):
        for lo, hi in segments:
            line = [src[r - 1 + k, lo:hi, :] for k in range(count + 2)]
            for k in range(count):
                q = r + k
                around = (line[k] + line[k + 2]) + (
                    src[q, lo - 1 : hi - 1, :] + src[q, lo + 1 : hi + 1, :]
                )
                dst[q, lo:hi, :] = 0.2 * line[k + 1] + w[q, lo:hi, :] * (f[q, lo:hi, :] + around)

    whole = (last - first) // per
    if whole > 1:

        def group(g, carry):
            some(first + g * per, per)
            return carry

        lax.fori_loop(0, whole, group, 0)
        first = first + whole * per
    for r in range(first, last, per):
        some(r, min(per, last - r))


def defect_sum(v, f, a4, first, lo, hi):
    total = None
    line = [v[first - 1 + k, lo:hi, :] for k in range(RATIO + 2)]
    for k in range(RATIO):
        q = first + k
        around = (line[k] + line[k + 2]) + (v[q, lo - 1 : hi - 1, :] + v[q, lo + 1 : hi + 1, :])
        one = (f[q, lo:hi, :] + around) - a4[q, lo:hi, :] * line[k + 1]
        total = one if total is None else total + one
    return total


def prepare(load, start, mass, u, f, w, a4, v1, v2, v3, cl, token, load_in, start_in, line, sems):
    copies = [
        pltpu.make_async_copy(load, load_in, sems.at[0]),
        pltpu.make_async_copy(start, start_in, sems.at[1]),
    ]
    for c in copies:
        c.start()

    def weights(r):
        a = 4.0 + mass[r]
        a4[R0 + r, C0:C1, :] = a
        w[R0 + r, C0:C1, :] = 0.8 / a

    loop(N, 2, weights)
    for c in copies:
        c.wait()

    def place(r):
        f[R0 + r, C0:C1, :] = load_in[r]
        u[R0 + r, C0:C1, :] = start_in[r]

    loop(N, 2, place)
    sweep_rows(u, v1, w, f, R0 + 1, R1 - 1, FULL)
    sweep_rows(v1, v2, w, f, R0 + 2, R1 - 2, FULL)
    sweep_rows(v2, v3, w, f, R0 + 3, R1 - 3, FULL)

    def block(i, carry):
        cl[i] = gather_columns(line, defect_sum(v3, f, a4, R0 + RATIO * i, C0, C1))
        return carry

    lax.fori_loop(1, C - 1, block, 0)
    token[...] = jnp.zeros((8, L), f32)


def before(u_in, f_in, w_in, v1_in, v2_in, v3_in, cl_in, a4, cm, re, ro, be, bo, ce, co, u, f, w, v1, v2, v3, cl, mext, l_even, l_odd, mb_even, mb_odd, wl, wr, wc, line):
    del u_in, f_in, w_in, v1_in, v2_in, v3_in, cl_in

    def lanes(left, right):
        for msg, out in ((left, wl), (right, wr)):
            out[...] = weight(msg[AT_MASS:FINE, :])
        for msg, out, cs, cf in ((left, wl, C0 - DS, C0 - DF), (right, wr, C1, C1)):

            def group(g, carry):
                s0, f0 = pl.multiple_of(g * (8 * DS), 8), pl.multiple_of(g * (8 * DF), 8)
                for r in range(8):
                    row = R0 + g * 8 + r
                    u[row, cs : cs + DS, :] = msg[pl.ds(s0 + r * DS, DS), :]
                    f[row, cf : cf + DF, :] = msg[pl.ds(AT_LOAD + f0 + r * DF, DF), :]
                    w[row, cf : cf + DF, :] = out[pl.ds(f0 + r * DF, DF), :]
                return carry

            lax.fori_loop(0, N // 8, group, 0)
        for i in range(C):
            mext[CR0 + i, CC0 : CC0 + C, :] = cm[i]
        place_coarse_lanes(mext, left, right, FINE)

    lane_even, band_even = parity("lane"), parity("band")
    either(lane_even, lambda: lanes(ro, re), lambda: lanes(re, ro))

    def bands(above, below, above_c, below_c):
        own = slice(C0, C1)
        for msg, row in ((above, R0), (below, R1)):
            first = row - DS if row == R0 else row
            for k in range(DS):
                u[first + k, own, :] = msg[k]
            first = row - DF if row == R0 else row
            for k in range(DF):
                f[first + k, own, :] = msg[DS + k]
                w[first + k, own, :] = weight(msg[DS + DF + k])
        for msg, first in ((above_c, R0 - DF), (below_c, R1)):
            half = DF * DEPTH
            wc[...] = weight(msg[...])
            for at, cs, cf in ((0, C0 - DS, C0 - DF), (half, C1, C1)):
                for k in range(DF):
                    row = first + k
                    s0, l0, m0 = at + k * DS, at + DF * DS + k * DF, at + DF * (DS + DF) + k * DF
                    u[row, cs : cs + DS, :] = msg[s0 : s0 + DS, :]
                    f[row, cf : cf + DF, :] = msg[l0 : l0 + DF, :]
                    w[row, cf : cf + DF, :] = wc[m0 : m0 + DF, :]

    either(band_even, lambda: bands(bo, be, co, ce), lambda: bands(be, bo, ce, co))

    for src, dst, k in ((u, v1, 1), (v1, v2, 2), (v2, v3, 3)):
        reach = BEFORE + 1 - k
        sweep_rows(src, dst, w, f, R0 - reach, R0 + k, FULL)
        sweep_rows(src, dst, w, f, R1 - k, R1 + reach, FULL)
        sweep_rows(src, dst, w, f, R0 + k, R1 - k, EDGES)

    for i in (0, C - 1):
        cl[i] = gather_columns(line, defect_sum(v3, f, a4, R0 + RATIO * i, C0, C1))

    def rims(i, carry):
        row = R0 + RATIO * i
        left = defect_sum(v3, f, a4, row, C0 - 4, C0 + 4)
        right = defect_sum(v3, f, a4, row, C1 - 4, C1 + 4)
        cl[i, 0:1, :] = jnp.sum(left[4:8, :], axis=0, keepdims=True) * (1.0 / RATIO)
        cl[i, C - 1 : C, :] = jnp.sum(right[0:4, :], axis=0, keepdims=True) * (1.0 / RATIO)
        return carry

    lax.fori_loop(1, C - 1, rims, 0)

    def out_lanes(right, left):
        pack_coarse_lanes(cl, right, left, 0)

        def group(g, carry):
            base = pl.multiple_of(g * 8, 8)
            for r in range(8):
                row = R0 + g * 8 + r
                right[pl.ds(LANE_COARSE + base + r, 1), :] = v3[row, C1 - 2 : C1 - 1, :]
                left[pl.ds(LANE_COARSE + base + r, 1), :] = v3[row, C0 + 1 : C0 + 2, :]
            return carry

        lax.fori_loop(0, N // 8, group, 0)

    either(lane_even, lambda: out_lanes(l_even, l_odd), lambda: out_lanes(l_odd, l_even))

    def out_bands(down, up):
        pack_coarse_bands(mext, down, up)
        for dst, rim, edge in ((down, R1 - 2, R1 - 1), (up, R0 + 1, R0)):
            at = BAND_COARSE
            dst[at : at + N, :] = v3[rim, C0:C1, :]
            dst[at + N : at + N + 8, :] = jnp.zeros((8, L), f32)
            dst[at + N : at + N + 1, :] = v3[edge, C0 - 1 : C0, :]
            dst[at + N + 1 : at + N + 2, :] = v3[edge, C1 : C1 + 1, :]

    either(band_even, lambda: out_bands(mb_even, mb_odd), lambda: out_bands(mb_odd, mb_even))


def coarse_bands(cl, re, ro, lext, b_even, b_odd):
    for i in range(C):
        lext[CR0 + i, CC0 : CC0 + C, :] = cl[i]
    either(
        parity("lane"),
        lambda: place_coarse_lanes(lext, ro, re, 0),
        lambda: place_coarse_lanes(lext, re, ro, 0),
    )
    either(
        parity("band"),
        lambda: pack_coarse_bands(lext, b_even, b_odd),
        lambda: pack_coarse_bands(lext, b_odd, b_even),
    )


def between(v_in, mext, mbe, mbo, le, lo, v, wext, ext):
    del v_in

    def lanes(left, right):
        def group(g, carry):
            base = pl.multiple_of(g * 8, 8)
            for r in range(8):
                row = R0 + g * 8 + r
                v[row, C0 - 2 : C0 - 1, :] = left[pl.ds(LANE_COARSE + base + r, 1), :]
                v[row, C1 + 1 : C1 + 2, :] = right[pl.ds(LANE_COARSE + base + r, 1), :]
            return carry

        lax.fori_loop(0, N // 8, group, 0)

    either(parity("lane"), lambda: lanes(lo, le), lambda: lanes(le, lo))
    span = slice(CC0 - H, CC0 + C + H)
    for i in range(C):
        ext[CR0 + i, span, :] = mext[CR0 + i, span, :]

    def bands(above, below):
        place_coarse_bands(ext, above, below)
        for msg, rim, edge in ((above, R0 - 2, R0 - 1), (below, R1 + 1, R1)):
            at = BAND_COARSE
            v[rim, C0:C1, :] = msg[at : at + N, :]
            v[edge, C0 - 1 : C0, :] = msg[at + N : at + N + 1, :]
            v[edge, C1 : C1 + 1, :] = msg[at + N + 1 : at + N + 2, :]

    either(parity("band"), lambda: bands(mbo, mbe), lambda: bands(mbe, mbo))

    def weights(r):
        wext[r] = weight(ext[r])

    loop(CR, 2, weights)


def after(v, f, w, wext, lext_in, lbe, lbo, out, lext, a, b, wide, t, s):
    span = slice(CC0 - H, CC0 + C + H)
    for i in range(C):
        lext[CR0 + i, span, :] = lext_in[CR0 + i, span, :]
    either(
        parity("band"),
        lambda: place_coarse_bands(lext, lbo, lbe),
        lambda: place_coarse_bands(lext, lbe, lbo),
    )

    def first(r):
        a[r] = wext[r] * lext[r]

    loop(CR, 2, first)
    src, dst = a, b
    for k in range(1, INNER):
        segments = ((8, 24), (24, 48)) if k <= 8 else ((16, 40),)
        sweep_rows(src, dst, wext, lext, k, CR - k, segments)
        src, dst = dst, src
    for i in range(-1, C + 1):
        row = src[CR0 + i, CC0 - 1 : CC0 + C + 1, :]
        for k in range(RATIO):
            wide[pl.ds(k, C + 2, stride=RATIO), :] = row
        for k in range(RATIO):
            q = i * RATIO + k
            if -AFTER <= q < N + AFTER:
                t[R0 + q, C0 - 4 : C1 + 4, :] = v[R0 + q, C0 - 4 : C1 + 4, :] + wide[...]
    sweep_rows(t, s, w, f, R0 - 1, R1 + 1, FULL, per=2)

    def last(r, carry):
        for lo, hi in ((0, 32), (32, 64)):
            line = [s[R0 + 4 * r - 1 + k, C0 + lo : C0 + hi, :] for k in range(6)]
            for k in range(4):
                q = R0 + 4 * r + k
                around = (line[k] + line[k + 2]) + (
                    s[q, C0 + lo - 1 : C0 + hi - 1, :] + s[q, C0 + lo + 1 : C0 + hi + 1, :]
                )
                out[4 * r + k, lo:hi, :] = 0.2 * line[k + 1] + w[q, C0 + lo : C0 + hi, :] * (
                    f[q, C0 + lo : C0 + hi, :] + around
                )
        return carry

    lax.fori_loop(0, N // 4, last, 0)


def swap_even(x, axis):
    n = lax.axis_size(axis)
    return lax.ppermute(x, axis, [(i, i ^ 1) for i in range(n)])


def swap_odd(x, axis):
    n = lax.axis_size(axis)
    return lax.ppermute(x, axis, [(i, (i + 1) % n if i % 2 else (i - 1) % n) for i in range(n)])


def shards(load, start, mass):
    load, start, mass = (pltpu.with_memory_space_constraint(x, pltpu.HBM) for x in (load, start, mass))
    dma = pltpu.SemaphoreType.DMA
    own, fine = sds(N, N, L), sds(ROWS, COLS, L)
    corner = sds(2 * DF * DEPTH, L)
    lane_msg, band_msg = sds(FINE + LANE_COARSE, L), sds(DEPTH, N, L)
    lane_coarse, band_coarse = sds(LANE_COARSE + N, L), sds(BAND_COARSE, L)
    band_both = sds(BAND_COARSE + BAND_RIM, L)
    coarse, own_coarse = sds(CR, CCOLS, L), sds(C, C, L)
    coarse_buf, fine_buf = pltpu.VMEM((CR, CCOLS, L), f32), pltpu.VMEM((ROWS, COLS, L), f32)
    own_buf, line = pltpu.VMEM((N, N, L), f32), pltpu.VMEM((N, L), f32)

    me, mo, be, bo, mass_in, cm = call(
        pack_fine,
        [lane_msg, lane_msg, band_msg, band_msg, own, own_coarse],
        [HBM] * 3,
        [pltpu.VMEM((2, 2, N, 8, L), f32), pltpu.VMEM((2, N, L), f32), dma((2, 2)), dma((1,)), dma((2, 3))],
        name="pack_fine",
    )(load, start, mass)
    ro, re = swap_odd(mo, "lane"), swap_even(me, "lane")
    rbo, rbe = swap_odd(bo, "band"), swap_even(be, "band")

    u, f, w, a4, v1, v2, v3, cl, token = call(
        prepare,
        [fine] * 7 + [own_coarse, sds(8, L)],
        [HBM, HBM, VM],
        [own_buf, own_buf, line, dma((2,))],
        flops=10**8,
        name="prepare",
    )(load, start, mass_in)

    ce, co = call(pack_corners, [corner, corner], [VM] * 3, name="pack_corners")(re, ro, token)
    rco, rce = swap_odd(co, "band"), swap_even(ce, "band")

    u, f, w, v1, v2, v3, cl, mext, le, lo, mbe, mbo = call(
        before,
        [fine] * 6 + [own_coarse, coarse, lane_coarse, lane_coarse, band_both, band_both],
        [VM] * 15,
        [pltpu.VMEM((N * DF, L), f32), pltpu.VMEM((N * DF, L), f32), pltpu.VMEM(corner.shape, f32), line],
        aliases={k: k for k in range(7)},
        flops=10**8,
        name="before",
    )(u, f, w, v1, v2, v3, cl, a4, cm, re, ro, rbe, rbo, rce, rco)
    rlo, rle = swap_odd(lo, "lane"), swap_even(le, "lane")
    rmbo, rmbe = swap_odd(mbo, "band"), swap_even(mbe, "band")

    lext, lbe, lbo = call(
        coarse_bands, [coarse, band_coarse, band_coarse], [VM] * 3, name="coarse_bands"
    )(cl, rle, rlo)
    rlbo, rlbe = swap_odd(lbo, "band"), swap_even(lbe, "band")
    v3, wext = call(
        between,
        [fine, coarse],
        [VM] * 6,
        [coarse_buf],
        aliases={0: 0},
        flops=10**7,
        name="between",
    )(v3, mext, rmbe, rmbo, rle, rlo)

    (out,) = call(
        after,
        [own],
        [VM] * 7,
        [coarse_buf] * 3 + [pltpu.VMEM((N + 8, L), f32), fine_buf, fine_buf],
        flops=10**8,
        name="after",
        inner=False,
    )(v3, f, w, wext, lext, rlbe, rlbo)
    return out


def solution(mesh):
    spec = P("band", "lane", None)
    return jax.shard_map(
        shards, mesh=mesh, in_specs=(spec, spec, spec), out_specs=spec, check_vma=False
    )
```

profile of v0, /device:TPU:1, one launch (start us, length us, event | category | flops | bytes accessed | tf_op | source)
XLA Modules:
  0.0 75.6 jit_solution(304858579936772853)
XLA Ops:
  0.0 2.5 %pack_fine.1 = (f32[848,128]{1,0:T(8,128)S(1)}, f32[848,128]{1,0:T(8,128)S(1)}, f32[10,64,128]{2,1,0:T(8,128)S(1)}, f32[10,64,128]{2,1,0:T(8,128)S(1)}, f32[64,6...) custom-call(f32[64,64,128]{2,1,0:T(8,128)} %load.3, f32[64,64,128]{2,1,0:T(8,128)} %start.3, f32[64,64,128]{2,1,0:T(8,128)} %mass_hbm.1), custom_call_target="tpu_custom_call" | custom-call | flops 1000000 | bytes 8000000 | tf_op jit(solution)/shard_map/pack_fine/pallas_call | solution.py:498
  2.5 2.1 %collective-permute-start = (f32[848,128]{1,0:T(8,128)S(1)}, f32[848,128]{1,0:T(8,128)S(1)}, u32[]{:S(2)}, u32[]{:S(2)}) collective-permute-start(f32[848,128]{1,0:T(8,128)S(1)} %get-tuple-element.46), channel_id=1, source_target_pairs={{0,1},{1,0},{2,3},{3,2},{4,5},{5,4},{6,7},{7,6},{8,9},{9,8},{10,11... | collective-permute-start | bytes 1302536 | tf_op jit(solution)/shard_map/ppermute | solution.py:478
  4.6 10.9 %collective-permute-start.1 = (f32[848,128]{1,0:T(8,128)S(1)}, f32[848,128]{1,0:T(8,128)S(1)}, u32[]{:S(2)}, u32[]{:S(2)}) collective-permute-start(f32[848,128]{1,0:T(8,128)S(1)} %get-tuple-element.47), channel_id=1, source_target_pairs={{0,31},{1,2},{2,1},{3,4},{4,3},{5,6},{6,5},{7,8},{8,7},{9,10},{10,... | collective-permute-start | bytes 1302536 | tf_op jit(solution)/shard_map/ppermute | solution.py:483
  15.5 1.2 %collective-permute-start.2 = (f32[10,64,128]{2,1,0:T(8,128)S(1)}, f32[10,64,128]{2,1,0:T(8,128)S(1)}, u32[]{:S(2)}, u32[]{:S(2)}) collective-permute-start(f32[10,64,128]{2,1,0:T(8,128)S(1)} %get-tuple-element.48), channel_id=1, source_target_pairs={{0,32},{32,0},{64,96},{96,64},{128,160},{160,128},{192,224},{224,1... | collective-permute-start | bytes 983048 | tf_op jit(solution)/shard_map/ppermute | solution.py:478
  16.7 0.6 collective-permute-start.3
  17.3 5.7 %prepare.1 = (f32[72,88,128]{2,1,0:T(8,128)S(1)}, f32[72,88,128]{2,1,0:T(8,128)S(1)}, f32[72,88,128]{2,1,0:T(8,128)S(1)}, f32[72,88,128]{2,1,0:T(8,128)S(1)}, f3...) custom-call(f32[64,64,128]{2,1,0:T(8,128)} %load.3, ...), custom_call_target="tpu_custom_call" | custom-call | flops 100000000 | bytes 8000000 | tf_op jit(solution)/shard_map/prepare/pallas_call | solution.py:508
  23.1 0.0 collective-permute-done.m_even.re
  23.1 8.6 %collective-permute-done.1.m_odd.ro = f32[848,128]{1,0:T(8,128)S(1)} collective-permute-done((f32[848,128]{1,0:T(8,128)S(1)}, f32[848,128]{1,0:T(8,128)S(1)}, u32[]{:S(2)}, u32[]{:S(2)}) %collective-permute-start.1) | collective-permute-done | bytes 434208 | tf_op jit(solution)/shard_map/ppermute | solution.py:483
  31.7 4.7 %collective-permute-start.4 = (f32[60,128]{1,0:T(8,128)S(1)}, f32[60,128]{1,0:T(8,128)S(1)}, u32[]{:S(2)}, u32[]{:S(2)}) collective-permute-start(f32[60,128]{1,0:T(8,128)S(1)} %get-tuple-element.51), channel_id=1, source_target_pairs={{0,32},{32,0},{64,96},{96,64},{128,160},{160,128},{192,224},{224,1... | collective-permute-start | bytes 92168 | tf_op jit(solution)/shard_map/ppermute | solution.py:478
  36.4 0.7 collective-permute-start.5
  37.1 0.0 collective-permute-done.2.be
  37.1 6.0 %collective-permute-done.3.bo = f32[10,64,128]{2,1,0:T(8,128)S(1)} collective-permute-done((f32[10,64,128]{2,1,0:T(8,128)S(1)}, f32[10,64,128]{2,1,0:T(8,128)S(1)}, u32[]{:S(2)}, u32[]{:S(2)}) %collective-permute-start.3) | collective-permute-done | bytes 327712 | tf_op jit(solution)/shard_map/ppermute | solution.py:483
  43.2 0.0 collective-permute-done.4.ce
  43.2 0.3 collective-permute-done.5.co
  43.5 2.0 %before.1 = (f32[72,88,128]{2,1,0:T(8,128)S(1)}, f32[72,88,128]{2,1,0:T(8,128)S(1)}, f32[72,88,128]{2,1,0:T(8,128)S(1)}, f32[72,88,128]{2,1,0:T(8,128)S(1)}, f32...) custom-call(f32[72,88,128]{2,1,0:T(8,128)S(1)} %get-tuple-element.37, ...), custom_call_target="tpu_custom_call", output_to_operand_aliasing={{0}: (0, {}), {1}: (1, {}), {2}: (2, {}), {3}: (3, {}), {4}... | custom-call | flops 100000000 | bytes 8000000 | tf_op jit(solution)/shard_map/before/pallas_call | solution.py:520
  45.5 0.1 collective-permute-start.8
  45.6 6.8 %collective-permute-start.9 = (f32[272,128]{1,0:T(8,128)S(1)}, f32[272,128]{1,0:T(8,128)S(1)}, u32[]{:S(2)}, u32[]{:S(2)}) collective-permute-start(f32[272,128]{1,0:T(8,128)S(1)} %get-tuple-element.58), channel_id=1, source_target_pairs={{0,31},{1,2},{2,1},{3,4},{4,3},{5,6},{6,5},{7,8},{8,7},{9,10},{10,... | collective-permute-start | bytes 417800 | tf_op jit(solution)/shard_map/ppermute | solution.py:483
  52.4 2.2 %collective-permute-start.6 = (f32[464,128]{1,0:T(8,128)S(1)}, f32[464,128]{1,0:T(8,128)S(1)}, u32[]{:S(2)}, u32[]{:S(2)}) collective-permute-start(f32[464,128]{1,0:T(8,128)S(1)} %get-tuple-element.55), channel_id=1, source_target_pairs={{0,32},{32,0},{64,96},{96,64},{128,160},{160,128},{192,224},{224,1... | collective-permute-start | bytes 712712 | tf_op jit(solution)/shard_map/ppermute | solution.py:478
  54.6 0.0 collective-permute-start.7
  54.6 0.0 collective-permute-done.8.le.re
  54.6 6.9 %collective-permute-done.9.lo.ro = f32[272,128]{1,0:T(8,128)S(1)} collective-permute-done((f32[272,128]{1,0:T(8,128)S(1)}, f32[272,128]{1,0:T(8,128)S(1)}, u32[]{:S(2)}, u32[]{:S(2)}) %collective-permute-start.9) | collective-permute-done | bytes 139296 | tf_op jit(solution)/shard_map/ppermute | solution.py:483
  61.5 0.1 coarse_bands.1
  61.5 0.5 collective-permute-start.10
  62.0 0.9 %collective-permute-start.11 = (f32[392,128]{1,0:T(8,128)S(1)}, f32[392,128]{1,0:T(8,128)S(1)}, u32[]{:S(2)}, u32[]{:S(2)}) collective-permute-start(f32[392,128]{1,0:T(8,128)S(1)} %get-tuple-element.66), channel_id=1, source_target_pairs={{0,224},{32,64},{64,32},{96,128},{128,96},{160,192},{192,160},{224... | collective-permute-start | bytes 602120 | tf_op jit(solution)/shard_map/ppermute | solution.py:483
  62.9 0.0 collective-permute-done.6.mbe
  62.9 2.4 %collective-permute-done.7.mbo = f32[464,128]{1,0:T(8,128)S(1)} collective-permute-done((f32[464,128]{1,0:T(8,128)S(1)}, f32[464,128]{1,0:T(8,128)S(1)}, u32[]{:S(2)}, u32[]{:S(2)}) %collective-permute-start.7) | collective-permute-done | bytes 237600 | tf_op jit(solution)/shard_map/ppermute | solution.py:483
  65.3 0.5 between.1
  65.8 0.0 collective-permute-done.10.lbe
  65.8 3.8 %collective-permute-done.11.lbo = f32[392,128]{1,0:T(8,128)S(1)} collective-permute-done((f32[392,128]{1,0:T(8,128)S(1)}, f32[392,128]{1,0:T(8,128)S(1)}, u32[]{:S(2)}, u32[]{:S(2)}) %collective-permute-start.11) | collective-permute-done | bytes 200736 | tf_op jit(solution)/shard_map/ppermute | solution.py:483
  69.6 6.0 %after.1 = f32[64,64,128]{2,1,0:T(8,128)} custom-call(f32[72,88,128]{2,1,0:T(8,128)S(1)} %get-tuple-element.59.v, f32[72,88,128]{2,1,0:T(8,128)S(1)} %get-tuple-element.60.f, f32[72,88,128]{2,1,0:T(8,128)S(1)} %get-tuple-element.61.w, f32[42,56,128]{2,1,0:T(8,128)S(1)} %get-tuple-element.62.wext, f32[42,56,128]{2,1,0:T(8,128)S(1)} %get-tuple-element.64.lext_in, ...), custom_call_target="tpu_custom_call" | custom-call | flops 100000000 | bytes 8000000 | tf_op jit(solution)/shard_map/after/pallas_call | solution.py:546
  (1 shorter events, 0.0 us)
Async XLA Ops:
  2.5 20.6 %collective-permute-start = (f32[848,128]{1,0:T(8,128)S(1)}, f32[848,128]{1,0:T(8,128)S(1)}, u32[]{:S(2)}, u32[]{:S(2)}) collective-permute-start(f32[848,128]{1,0:T(8,128)S(1)} %get-tuple-element.46), channel_id=1, source_target_pairs={{0,1},{1,0},{2,3},{3,2},{4,5},{5,4},{6,7},{7,6},{8,9},{9,8},{10,11... | collective-permute-start | bytes 1302536 | tf_op jit(solution)/shard_map/ppermute | solution.py:478
  4.6 27.1 %collective-permute-start.1 = (f32[848,128]{1,0:T(8,128)S(1)}, f32[848,128]{1,0:T(8,128)S(1)}, u32[]{:S(2)}, u32[]{:S(2)}) collective-permute-start(f32[848,128]{1,0:T(8,128)S(1)} %get-tuple-element.47), channel_id=1, source_target_pairs={{0,31},{1,2},{2,1},{3,4},{4,3},{5,6},{6,5},{7,8},{8,7},{9,10},{10,... | collective-permute-start | bytes 1302536 | tf_op jit(solution)/shard_map/ppermute | solution.py:483
  15.5 21.6 %collective-permute-start.2 = (f32[10,64,128]{2,1,0:T(8,128)S(1)}, f32[10,64,128]{2,1,0:T(8,128)S(1)}, u32[]{:S(2)}, u32[]{:S(2)}) collective-permute-start(f32[10,64,128]{2,1,0:T(8,128)S(1)} %get-tuple-element.48), channel_id=1, source_target_pairs={{0,32},{32,0},{64,96},{96,64},{128,160},{160,128},{192,224},{224,1... | collective-permute-start | bytes 983048 | tf_op jit(solution)/shard_map/ppermute | solution.py:478
  16.7 26.4 %collective-permute-start.3 = (f32[10,64,128]{2,1,0:T(8,128)S(1)}, f32[10,64,128]{2,1,0:T(8,128)S(1)}, u32[]{:S(2)}, u32[]{:S(2)}) collective-permute-start(f32[10,64,128]{2,1,0:T(8,128)S(1)} %get-tuple-element.49), channel_id=1, source_target_pairs={{0,224},{32,64},{64,32},{96,128},{128,96},{160,192},{192,160},{224... | collective-permute-start | bytes 983048 | tf_op jit(solution)/shard_map/ppermute | solution.py:483
  31.7 11.4 %collective-permute-start.4 = (f32[60,128]{1,0:T(8,128)S(1)}, f32[60,128]{1,0:T(8,128)S(1)}, u32[]{:S(2)}, u32[]{:S(2)}) collective-permute-start(f32[60,128]{1,0:T(8,128)S(1)} %get-tuple-element.51), channel_id=1, source_target_pairs={{0,32},{32,0},{64,96},{96,64},{128,160},{160,128},{192,224},{224,1... | collective-permute-start | bytes 92168 | tf_op jit(solution)/shard_map/ppermute | solution.py:478
  36.4 7.1 %collective-permute-start.5 = (f32[60,128]{1,0:T(8,128)S(1)}, f32[60,128]{1,0:T(8,128)S(1)}, u32[]{:S(2)}, u32[]{:S(2)}) collective-permute-start(f32[60,128]{1,0:T(8,128)S(1)} %get-tuple-element.52), channel_id=1, source_target_pairs={{0,224},{32,64},{64,32},{96,128},{128,96},{160,192},{192,160},{224... | collective-permute-start | bytes 92168 | tf_op jit(solution)/shard_map/ppermute | solution.py:483
  45.5 9.1 %collective-permute-start.8 = (f32[272,128]{1,0:T(8,128)S(1)}, f32[272,128]{1,0:T(8,128)S(1)}, u32[]{:S(2)}, u32[]{:S(2)}) collective-permute-start(f32[272,128]{1,0:T(8,128)S(1)} %get-tuple-element.57), channel_id=1, source_target_pairs={{0,1},{1,0},{2,3},{3,2},{4,5},{5,4},{6,7},{7,6},{8,9},{9,8},{10,11... | collective-permute-start | bytes 417800 | tf_op jit(solution)/shard_map/ppermute | solution.py:478
  45.6 15.9 %collective-permute-start.9 = (f32[272,128]{1,0:T(8,128)S(1)}, f32[272,128]{1,0:T(8,128)S(1)}, u32[]{:S(2)}, u32[]{:S(2)}) collective-permute-start(f32[272,128]{1,0:T(8,128)S(1)} %get-tuple-element.58), channel_id=1, source_target_pairs={{0,31},{1,2},{2,1},{3,4},{4,3},{5,6},{6,5},{7,8},{8,7},{9,10},{10,... | collective-permute-start | bytes 417800 | tf_op jit(solution)/shard_map/ppermute | solution.py:483
  52.4 10.5 %collective-permute-start.6 = (f32[464,128]{1,0:T(8,128)S(1)}, f32[464,128]{1,0:T(8,128)S(1)}, u32[]{:S(2)}, u32[]{:S(2)}) collective-permute-start(f32[464,128]{1,0:T(8,128)S(1)} %get-tuple-element.55), channel_id=1, source_target_pairs={{0,32},{32,0},{64,96},{96,64},{128,160},{160,128},{192,224},{224,1... | collective-permute-start | bytes 712712 | tf_op jit(solution)/shard_map/ppermute | solution.py:478
  54.6 10.7 %collective-permute-start.7 = (f32[464,128]{1,0:T(8,128)S(1)}, f32[464,128]{1,0:T(8,128)S(1)}, u32[]{:S(2)}, u32[]{:S(2)}) collective-permute-start(f32[464,128]{1,0:T(8,128)S(1)} %get-tuple-element.56), channel_id=1, source_target_pairs={{0,224},{32,64},{64,32},{96,128},{128,96},{160,192},{192,160},{224... | collective-permute-start | bytes 712712 | tf_op jit(solution)/shard_map/ppermute | solution.py:483
  61.5 4.3 %collective-permute-start.10 = (f32[392,128]{1,0:T(8,128)S(1)}, f32[392,128]{1,0:T(8,128)S(1)}, u32[]{:S(2)}, u32[]{:S(2)}) collective-permute-start(f32[392,128]{1,0:T(8,128)S(1)} %get-tuple-element.65), channel_id=1, source_target_pairs={{0,32},{32,0},{64,96},{96,64},{128,160},{160,128},{192,224},{224,1... | collective-permute-start | bytes 602120 | tf_op jit(solution)/shard_map/ppermute | solution.py:478
  62.0 7.6 %collective-permute-start.11 = (f32[392,128]{1,0:T(8,128)S(1)}, f32[392,128]{1,0:T(8,128)S(1)}, u32[]{:S(2)}, u32[]{:S(2)}) collective-permute-start(f32[392,128]{1,0:T(8,128)S(1)} %get-tuple-element.66), channel_id=1, source_target_pairs={{0,224},{32,64},{64,32},{96,128},{128,96},{160,192},{192,160},{224... | collective-permute-start | bytes 602120 | tf_op jit(solution)/shard_map/ppermute | solution.py:483
where the time goes:
time: 75.7 us; the launch traced here: 75.6 us
  starting transfers between devices  30.7 us (41%)
  waiting for transfers between devices  28.1 us (37%)
  Pallas kernels  16.8 us (22%)
    ppermute x6, waiting for transfers between devices, swap_odd(): lax.ppermute(x, axis, [(i, (i + 1) % n if i % 2 else (i - 1) % n) for i i...  28.1 us
    ppermute x6, starting transfers between devices, swap_odd(): lax.ppermute(x, axis, [(i, (i + 1) % n if i % 2 else (i - 1) % n) for i i...  19.9 us
    ppermute x6, starting transfers between devices, swap_even(): return lax.ppermute(x, axis, [(i, i ^ 1) for i in range(n)])  10.8 us
    pallas_call x1, Pallas kernels, shards(): call(after, [own], [VM] * 7, [coarse_buf] * 3 + [pltpu.VMEM((N + 8, L), f...  6.03 us
    pallas_call x1, Pallas kernels, shards(): call(prepare, [fine] * 7 + [own_coarse, sds(8, L)], [HBM, HBM, VM], [own_...  5.72 us
    pallas_call x1, Pallas kernels, shards(): call(pack_fine, [lane_msg, lane_msg, band_msg, band_msg, own, own_coarse]...  2.46 us
    pallas_call x1, Pallas kernels, shards(): call(before, [fine] * 6 + [own_coarse, coarse, lane_coarse, lane_coarse,...  1.99 us
  transfers between devices with their start and end apart: 12, of which 6 were waited for; matrix products, arithmetic and copies ran while one was open for 0% of the time, Pallas kernels for 8%

commit v1 on v0

--- a/solution.py
+++ b/solution.py
@@ -1,9 +1,12 @@
+import functools
+
 import jax
 import jax.numpy as jnp
 from jax import lax
 from jax.experimental import pallas as pl
 from jax.experimental.pallas import tpu as pltpu
 from jax.sharding import PartitionSpec as P
+
 
 RATIO = 4
 BEFORE = 3
@@ -21,7 +24,6 @@
 R0, C0 = DS, 12
 R1, C1 = R0 + N, C0 + N
 ROWS, COLS = R1 + DS, C1 + 12
-LEFT, RIGHT = slice(C0 - 4, C0 + 4), slice(C1 - 4, C1 + 4)
 FULL = ((C0 - 4, C0 + 20), (C0 + 20, C0 + 44), (C0 + 44, C0 + 68))
 EDGES = ((C0 - 4, C0 + 4), (C1 - 4, C1 + 4))
 H = INNER
@@ -32,6 +34,7 @@
 BAND_COARSE = -(-sum(WIDTHS) // 8) * 8
 BAND_RIM = N + 8
 LANE_COARSE = C * H
+PIECES = 4
 FIT = 16 * 2**20
 
 f32 = jnp.float32
@@ -59,17 +62,16 @@
 HBM = pl.BlockSpec(memory_space=pltpu.HBM)
 
 
-def call(body, outs, ins, scratch=(), aliases=None, flops=10**6, name=None, inner=True):
+def call(body, outs, ins, scratch=(), aliases=None, flops=10**6, result=False):
     return pl.pallas_call(
         body,
-        out_shape=[pltpu.VMEM(o.shape, o.dtype) for o in outs] if inner else outs,
+        out_shape=outs[:result] + [pltpu.VMEM(o.shape, o.dtype) for o in outs[result:]],
         in_specs=ins,
-        out_specs=[VM] * len(outs),
+        out_specs=[HBM] * result + [VM] * (len(outs) - result),
         scratch_shapes=list(scratch),
         input_output_aliases=aliases or {},
         compiler_params=pltpu.CompilerParams(vmem_limit_bytes=FIT),
         cost_estimate=pl.CostEstimate(flops=flops, bytes_accessed=8 * 10**6, transcendentals=0),
-        name=name,
     )
 
 
@@ -90,7 +92,7 @@
     return total * (1.0 / RATIO)
 
 
-def pack_fine(load, start, mass_hbm, m_even, m_odd, b_even, b_odd, mass, cm, side, line, sem_side, sem_mass, sem_band):
+def pack_fine(load, start, mass_hbm, m_even, m_odd, b_even, b_odd, mass, cm, edges, c_odd, side, line, sem_side, sem_mass, sem_band):
     whole = pltpu.make_async_copy(mass_hbm, mass, sem_mass.at[0])
     copies = []
     for k, src in enumerate((start, load)):
@@ -150,9 +152,21 @@
             return carry
 
         lax.fori_loop(0, N // 8, group, 0)
-        pack_coarse_lanes(cm, right, left, FINE)
-
-    either(lane_even, lambda: pack_mass(m_even, m_odd), lambda: pack_mass(m_odd, m_even))
+
+    either(
+        lane_even,
+        lambda: pack_mass(m_even, m_odd),
+        lambda: pack_mass(m_odd, m_even),
+    )
+    for i in range(C):
+        row = cm[i]
+        edges[i * H : (i + 1) * H, :] = row[:H, :]
+        edges[LANE_COARSE + i * H : LANE_COARSE + (i + 1) * H, :] = row[C - H :, :]
+
+    def odd_side(first):
+        c_odd[...] = edges[first : first + LANE_COARSE, :]
+
+    either(lane_even, lambda: odd_side(0), lambda: odd_side(LANE_COARSE))
     for c in bands:
         c.wait()
 
@@ -186,11 +200,10 @@
         left[lo : lo + H, :] = row[:H, :]
 
 
-def place_coarse_lanes(ext, left, right, at):
+def place_coarse_lanes(ext, left, right, at_left=0, at_right=0):
     for i in range(C):
-        lo = at + i * H
-        ext[CR0 + i, CC0 - H : CC0, :] = left[lo : lo + H, :]
-        ext[CR0 + i, CC0 + C : CC0 + C + H, :] = right[lo : lo + H, :]
+        ext[CR0 + i, CC0 - H : CC0, :] = left[at_left + i * H : at_left + (i + 1) * H, :]
+        ext[CR0 + i, CC0 + C : CC0 + C + H, :] = right[at_right + i * H : at_right + (i + 1) * H, :]
 
 
 def pack_coarse_bands(ext, down, up):
@@ -284,7 +297,7 @@
     token[...] = jnp.zeros((8, L), f32)
 
 
-def before(u_in, f_in, w_in, v1_in, v2_in, v3_in, cl_in, a4, cm, re, ro, be, bo, ce, co, u, f, w, v1, v2, v3, cl, mext, l_even, l_odd, mb_even, mb_odd, wl, wr, wc, line):
+def before(u_in, f_in, w_in, v1_in, v2_in, v3_in, cl_in, a4, re, ro, be, bo, ce, co, u, f, w, v1, v2, v3, cl, l_even, l_odd, rim_even, rim_odd, wl, wr, wc, line):
     del u_in, f_in, w_in, v1_in, v2_in, v3_in, cl_in
 
     def lanes(left, right):
@@ -302,9 +315,6 @@
                 return carry
 
             lax.fori_loop(0, N // 8, group, 0)
-        for i in range(C):
-            mext[CR0 + i, CC0 : CC0 + C, :] = cm[i]
-        place_coarse_lanes(mext, left, right, FINE)
 
     lane_even, band_even = parity("lane"), parity("band")
     either(lane_even, lambda: lanes(ro, re), lambda: lanes(re, ro))
@@ -367,30 +377,62 @@
     either(lane_even, lambda: out_lanes(l_even, l_odd), lambda: out_lanes(l_odd, l_even))
 
     def out_bands(down, up):
-        pack_coarse_bands(mext, down, up)
         for dst, rim, edge in ((down, R1 - 2, R1 - 1), (up, R0 + 1, R0)):
-            at = BAND_COARSE
+            at = 0
             dst[at : at + N, :] = v3[rim, C0:C1, :]
             dst[at + N : at + N + 8, :] = jnp.zeros((8, L), f32)
             dst[at + N : at + N + 1, :] = v3[edge, C0 - 1 : C0, :]
             dst[at + N + 1 : at + N + 2, :] = v3[edge, C1 : C1 + 1, :]
 
-    either(band_even, lambda: out_bands(mb_even, mb_odd), lambda: out_bands(mb_odd, mb_even))
-
-
-def coarse_bands(cl, re, ro, lext, b_even, b_odd):
+    either(band_even, lambda: out_bands(rim_even, rim_odd), lambda: out_bands(rim_odd, rim_even))
+
+
+def relay(edges, out):
+    def put(first):
+        out[...] = edges[first : first + LANE_COARSE, :]
+
+    either(parity("lane"), lambda: put(LANE_COARSE), lambda: put(0))
+
+
+def far(lane, lanes):
+    at = lax.rem(lane, lanes // 2)
+    return (at == 0) | (at == lanes // 2 - 1)
+
+
+def mass_bands(lanes, cm, edges, near, across, mext, b_even, b_odd):
+    for i in range(C):
+        mext[CR0 + i, CC0 : CC0 + C, :] = cm[i]
+
+    def place(odd):
+        either(
+            parity("lane"),
+            lambda: place_coarse_lanes(mext, odd, edges),
+            lambda: place_coarse_lanes(mext, edges, odd, LANE_COARSE),
+        )
+
+    either(far(lax.axis_index("lane"), lanes), lambda: place(across), lambda: place(near))
+    either(
+        parity("band"),
+        lambda: pack_coarse_bands(mext, b_even, b_odd),
+        lambda: pack_coarse_bands(mext, b_odd, b_even),
+    )
+
+
+def coarse_bands(cl, re, ro, rim_even, rim_odd, lext, b_even, b_odd):
     for i in range(C):
         lext[CR0 + i, CC0 : CC0 + C, :] = cl[i]
     either(
         parity("lane"),
-        lambda: place_coarse_lanes(lext, ro, re, 0),
-        lambda: place_coarse_lanes(lext, re, ro, 0),
+        lambda: place_coarse_lanes(lext, ro, re),
+        lambda: place_coarse_lanes(lext, re, ro),
     )
     either(
         parity("band"),
         lambda: pack_coarse_bands(lext, b_even, b_odd),
         lambda: pack_coarse_bands(lext, b_odd, b_even),
     )
+    b_even[BAND_COARSE:, :] = rim_even[...]
+    b_odd[BAND_COARSE:, :] = rim_odd[...]
 
 
 def between(v_in, mext, mbe, mbo, le, lo, v, wext, ext):
@@ -414,29 +456,30 @@
 
     def bands(above, below):
         place_coarse_bands(ext, above, below)
+
+    either(parity("band"), lambda: bands(mbo, mbe), lambda: bands(mbe, mbo))
+
+    def weights(r):
+        wext[r] = weight(ext[r])
+
+    loop(CR, 2, weights)
+
+
+def after(v_in, f, w, wext, lext_in, lbe, lbo, result, v, lext, a, b, wide, t, s, out, sems):
+    span = slice(CC0 - H, CC0 + C + H)
+    for i in range(C):
+        lext[CR0 + i, span, :] = lext_in[CR0 + i, span, :]
+    del v_in
+
+    def bands(above, below):
+        place_coarse_bands(lext, above, below)
         for msg, rim, edge in ((above, R0 - 2, R0 - 1), (below, R1 + 1, R1)):
             at = BAND_COARSE
             v[rim, C0:C1, :] = msg[at : at + N, :]
             v[edge, C0 - 1 : C0, :] = msg[at + N : at + N + 1, :]
             v[edge, C1 : C1 + 1, :] = msg[at + N + 1 : at + N + 2, :]
 
-    either(parity("band"), lambda: bands(mbo, mbe), lambda: bands(mbe, mbo))
-
-    def weights(r):
-        wext[r] = weight(ext[r])
-
-    loop(CR, 2, weights)
-
-
-def after(v, f, w, wext, lext_in, lbe, lbo, out, lext, a, b, wide, t, s):
-    span = slice(CC0 - H, CC0 + C + H)
-    for i in range(C):
-        lext[CR0 + i, span, :] = lext_in[CR0 + i, span, :]
-    either(
-        parity("band"),
-        lambda: place_coarse_bands(lext, lbo, lbe),
-        lambda: place_coarse_bands(lext, lbe, lbo),
-    )
+    either(parity("band"), lambda: bands(lbo, lbe), lambda: bands(lbe, lbo))
 
     def first(r):
         a[r] = wext[r] * lext[r]
@@ -470,7 +513,15 @@
                 )
         return carry
 
-    lax.fori_loop(0, N // 4, last, 0)
+    copies = []
+    for piece in range(PIECES):
+        rows = N // PIECES
+        lax.fori_loop(piece * rows // 4, (piece + 1) * rows // 4, last, 0)
+        span = pl.ds(piece * rows, rows)
+        copies.append(pltpu.make_async_copy(out.at[span], result.at[span], sems.at[piece]))
+        copies[-1].start()
+    for c in copies:
+        c.wait()
 
 
 def swap_even(x, axis):
@@ -488,22 +539,32 @@
     dma = pltpu.SemaphoreType.DMA
     own, fine = sds(N, N, L), sds(ROWS, COLS, L)
     corner = sds(2 * DF * DEPTH, L)
-    lane_msg, band_msg = sds(FINE + LANE_COARSE, L), sds(DEPTH, N, L)
+    lane_msg, band_msg = sds(FINE, L), sds(DEPTH, N, L)
+    rim, lane_mass = sds(BAND_RIM, L), sds(LANE_COARSE, L)
     lane_coarse, band_coarse = sds(LANE_COARSE + N, L), sds(BAND_COARSE, L)
     band_both = sds(BAND_COARSE + BAND_RIM, L)
     coarse, own_coarse = sds(CR, CCOLS, L), sds(C, C, L)
     coarse_buf, fine_buf = pltpu.VMEM((CR, CCOLS, L), f32), pltpu.VMEM((ROWS, COLS, L), f32)
     own_buf, line = pltpu.VMEM((N, N, L), f32), pltpu.VMEM((N, L), f32)
 
-    me, mo, be, bo, mass_in, cm = call(
+    me, mo, be, bo, mass_in, cm, edges, cmo = call(
         pack_fine,
-        [lane_msg, lane_msg, band_msg, band_msg, own, own_coarse],
+        [lane_msg, lane_msg, band_msg, band_msg, own, own_coarse, sds(2 * LANE_COARSE, L), lane_mass],
         [HBM] * 3,
         [pltpu.VMEM((2, 2, N, 8, L), f32), pltpu.VMEM((2, N, L), f32), dma((2, 2)), dma((1,)), dma((2, 3))],
-        name="pack_fine",
     )(load, start, mass)
+    rbo, rbe = swap_odd(bo, "band"), swap_even(be, "band")
     ro, re = swap_odd(mo, "lane"), swap_even(me, "lane")
-    rbo, rbe = swap_odd(bo, "band"), swap_even(be, "band")
+
+    n = lax.axis_size("lane")
+    half = n // 2
+    redges = swap_even(edges, "lane")
+    pairs = [(i, i + 1) for i in range(1, n - 1, 2) if i != half - 1]
+    rnear = lax.ppermute(cmo, "lane", pairs + [(j, i) for i, j in pairs])
+    (hand,) = call(relay, [lane_mass], [VM])(redges)
+    pairs = [(half - 2, half + 1), (n - 2, 1)]
+    rhand = lax.ppermute(hand, "lane", pairs + [(j, i) for i, j in pairs])
+    racross = swap_even(rhand, "lane")
 
     u, f, w, a4, v1, v2, v3, cl, token = call(
         prepare,
@@ -511,52 +572,48 @@
         [HBM, HBM, VM],
         [own_buf, own_buf, line, dma((2,))],
         flops=10**8,
-        name="prepare",
     )(load, start, mass_in)
 
-    ce, co = call(pack_corners, [corner, corner], [VM] * 3, name="pack_corners")(re, ro, token)
+    ce, co = call(pack_corners, [corner, corner], [VM] * 3)(re, ro, token)
     rco, rce = swap_odd(co, "band"), swap_even(ce, "band")
 
-    u, f, w, v1, v2, v3, cl, mext, le, lo, mbe, mbo = call(
+    mext, mbe, mbo = call(
+        functools.partial(mass_bands, n), [coarse, band_coarse, band_coarse], [VM] * 4
+    )(cm, redges, rnear, racross)
+    rmbo, rmbe = swap_odd(mbo, "band"), swap_even(mbe, "band")
+
+    u, f, w, v1, v2, v3, cl, le, lo, rime, rimo = call(
         before,
-        [fine] * 6 + [own_coarse, coarse, lane_coarse, lane_coarse, band_both, band_both],
-        [VM] * 15,
+        [fine] * 6 + [own_coarse, lane_coarse, lane_coarse, rim, rim],
+        [VM] * 14,
         [pltpu.VMEM((N * DF, L), f32), pltpu.VMEM((N * DF, L), f32), pltpu.VMEM(corner.shape, f32), line],
         aliases={k: k for k in range(7)},
         flops=10**8,
-        name="before",
-    )(u, f, w, v1, v2, v3, cl, a4, cm, re, ro, rbe, rbo, rce, rco)
+    )(u, f, w, v1, v2, v3, cl, a4, re, ro, rbe, rbo, rce, rco)
     rlo, rle = swap_odd(lo, "lane"), swap_even(le, "lane")
-    rmbo, rmbe = swap_odd(mbo, "band"), swap_even(mbe, "band")
-
     lext, lbe, lbo = call(
-        coarse_bands, [coarse, band_coarse, band_coarse], [VM] * 3, name="coarse_bands"
-    )(cl, rle, rlo)
+        coarse_bands, [coarse, band_both, band_both], [VM] * 5
+    )(cl, rle, rlo, rime, rimo)
     rlbo, rlbe = swap_odd(lbo, "band"), swap_even(lbe, "band")
     v3, wext = call(
-        between,
-        [fine, coarse],
-        [VM] * 6,
-        [coarse_buf],
-        aliases={0: 0},
-        flops=10**7,
-        name="between",
+        between, [fine, coarse], [VM] * 6, [coarse_buf], aliases={0: 0}, flops=10**7
     )(v3, mext, rmbe, rmbo, rle, rlo)
 
-    (out,) = call(
+    out, _ = call(
         after,
-        [own],
+        [own, fine],
         [VM] * 7,
-        [coarse_buf] * 3 + [pltpu.VMEM((N + 8, L), f32), fine_buf, fine_buf],
+        [coarse_buf] * 3 + [pltpu.VMEM((N + 8, L), f32), fine_buf, fine_buf, own_buf, dma((PIECES,))],
         flops=10**8,
-        name="after",
-        inner=False,
+        aliases={0: 1},
+        result=True,
     )(v3, f, w, wext, lext, rlbe, rlbo)
     return out
 
 
 def solution(mesh):
     spec = P("band", "lane", None)
+
     return jax.shard_map(
         shards, mesh=mesh, in_specs=(spec, spec, spec), out_specs=spec, check_vma=False
     )

time: 75.7 us -> 76.9 us (1.016)
  starting transfers between devices: 30.7 us -> 35.1 us
  waiting for transfers between devices: 28.1 us -> 25.1 us
    ppermute x6, waiting for transfers between devices: 28.1 us -> 25.1 us  [swap_odd(): lax.ppermute(x, axis, [(i, (i + 1) % n if i % 2 else (i - 1) % n) for i i...]
    ppermute x6, starting transfers between devices: 19.9 us -> 21.8 us  [swap_odd(): lax.ppermute(x, axis, [(i, (i + 1) % n if i % 2 else (i - 1) % n) for i i...]
    ppermute x0 -> x2, starting transfers between devices: none -> 1.32 us  [the longest x1 0.67 us: shards(): rhand = lax.ppermute(hand, 'lane', pairs + [(j, i) for i, j in pairs])]
    ppermute x6 -> x8, starting transfers between devices: 10.8 us -> 12 us  [swap_even(): return lax.ppermute(x, axis, [(i, i ^ 1) for i in range(n)])]
    pallas_call x5 -> x7, Pallas kernels: 10.6 us -> 10.3 us  [the longest x1 5.69 us: shards(): call(after, [own, fine], [VM] * 7, [coarse_buf] * 3 + [pltpu.VMEM((N + 8,...]
  transfers between devices with their start and end apart: 12 -> 16, of which waited for: 6 -> 5; matrix products, arithmetic and copies ran while one was open for 0% -> 0% of each run, Pallas kernels for 8% -> 11%
where the time goes in v1:
time: 76.9 us; the launch traced here: 76.8 us
  starting transfers between devices  35.1 us (46%)
  waiting for transfers between devices  25.1 us (33%)
  Pallas kernels  16.4 us (21%)
    ppermute x6, waiting for transfers between devices, swap_odd(): lax.ppermute(x, axis, [(i, (i + 1) % n if i % 2 else (i - 1) % n) for i i...  25.1 us
    ppermute x6, starting transfers between devices, swap_odd(): lax.ppermute(x, axis, [(i, (i + 1) % n if i % 2 else (i - 1) % n) for i i...  21.8 us
    ppermute x8, starting transfers between devices, swap_even(): return lax.ppermute(x, axis, [(i, i ^ 1) for i in range(n)])  12 us
    pallas_call x1, Pallas kernels, shards(): call(after, [own, fine], [VM] * 7, [coarse_buf] * 3 + [pltpu.VMEM((N + 8,...  5.69 us
    pallas_call x1, Pallas kernels, shards(): call(prepare, [fine] * 7 + [own_coarse, sds(8, L)], [HBM, HBM, VM], [own_...  5.68 us
    pallas_call x1, Pallas kernels, shards(): call(pack_fine, [lane_msg, lane_msg, band_msg, band_msg, own, own_coarse,...  2.47 us
    pallas_call x1, Pallas kernels, shards(): call(before, [fine] * 6 + [own_coarse, lane_coarse, lane_coarse, rim, rim...  1.92 us
  transfers between devices with their start and end apart: 16, of which 5 were waited for; matrix products, arithmetic and copies ran while one was open for 0% of the time, Pallas kernels for 11%

profile of v1, /device:TPU:1, one launch (start us, length us, event | category | flops | bytes accessed | tf_op | source)
XLA Modules:
  0.0 76.8 jit_solution(7545724185121299894)
XLA Ops:
  0.0 2.5 %shard_map.37 = (f32[640,128]{1,0:T(8,128)S(1)}, f32[640,128]{1,0:T(8,128)S(1)}, f32[10,64,128]{2,1,0:T(8,128)S(1)}, f32[10,64,128]{2,1,0:T(8,128)S(1)}, f32[64,...) custom-call(f32[64,64,128]{2,1,0:T(8,128)} %load.3, ...), custom_call_target="tpu_custom_call" | custom-call | flops 1000000 | bytes 8000000 | tf_op jit(solution)/shard_map/pallas_call | solution.py:550
  2.5 2.1 %collective-permute-start = (f32[640,128]{1,0:T(8,128)S(1)}, f32[640,128]{1,0:T(8,128)S(1)}, u32[]{:S(2)}, u32[]{:S(2)}) collective-permute-start(f32[640,128]{1,0:T(8,128)S(1)} %get-tuple-element.50), channel_id=1, source_target_pairs={{0,1},{1,0},{2,3},{3,2},{4,5},{5,4},{6,7},{7,6},{8,9},{9,8},{10,11... | collective-permute-start | bytes 983048 | tf_op jit(solution)/shard_map/ppermute | solution.py:529
  4.6 10.9 %collective-permute-start.1 = (f32[640,128]{1,0:T(8,128)S(1)}, f32[640,128]{1,0:T(8,128)S(1)}, u32[]{:S(2)}, u32[]{:S(2)}) collective-permute-start(f32[640,128]{1,0:T(8,128)S(1)} %get-tuple-element.51), channel_id=1, source_target_pairs={{0,31},{1,2},{2,1},{3,4},{4,3},{5,6},{6,5},{7,8},{8,7},{9,10},{10,... | collective-permute-start | bytes 983048 | tf_op jit(solution)/shard_map/ppermute | solution.py:534
  15.5 1.2 %collective-permute-start.2 = (f32[10,64,128]{2,1,0:T(8,128)S(1)}, f32[10,64,128]{2,1,0:T(8,128)S(1)}, u32[]{:S(2)}, u32[]{:S(2)}) collective-permute-start(f32[10,64,128]{2,1,0:T(8,128)S(1)} %get-tuple-element.52), channel_id=1, source_target_pairs={{0,32},{32,0},{64,96},{96,64},{128,160},{160,128},{192,224},{224,1... | collective-permute-start | bytes 983048 | tf_op jit(solution)/shard_map/ppermute | solution.py:529
  16.7 0.6 collective-permute-start.3
  17.3 0.0 collective-permute-start.6
  17.4 5.7 %shard_map.38 = (f32[72,88,128]{2,1,0:T(8,128)S(1)}, f32[72,88,128]{2,1,0:T(8,128)S(1)}, f32[72,88,128]{2,1,0:T(8,128)S(1)}, f32[72,88,128]{2,1,0:T(8,128)S(1)},...) custom-call(f32[64,64,128]{2,1,0:T(8,128)} %load.3, ...), custom_call_target="tpu_custom_call" | custom-call | flops 100000000 | bytes 8000000 | tf_op jit(solution)/shard_map/pallas_call | solution.py:569
  23.0 0.0 collective-permute-done.m_even.re
  23.0 1.1 %collective-permute-done.1.m_odd.ro = f32[640,128]{1,0:T(8,128)S(1)} collective-permute-done((f32[640,128]{1,0:T(8,128)S(1)}, f32[640,128]{1,0:T(8,128)S(1)}, u32[]{:S(2)}, u32[]{:S(2)}) %collective-permute-start.1) | collective-permute-done | bytes 327712 | tf_op jit(solution)/shard_map/ppermute | solution.py:534
  24.1 7.7 %collective-permute-start.4 = (f32[60,128]{1,0:T(8,128)S(1)}, f32[60,128]{1,0:T(8,128)S(1)}, u32[]{:S(2)}, u32[]{:S(2)}) collective-permute-start(f32[60,128]{1,0:T(8,128)S(1)} %get-tuple-element.55), channel_id=1, source_target_pairs={{0,32},{32,0},{64,96},{96,64},{128,160},{160,128},{192,224},{224,1... | collective-permute-start | bytes 92168 | tf_op jit(solution)/shard_map/ppermute | solution.py:529
  31.8 1.8 %collective-permute-start.5 = (f32[60,128]{1,0:T(8,128)S(1)}, f32[60,128]{1,0:T(8,128)S(1)}, u32[]{:S(2)}, u32[]{:S(2)}) collective-permute-start(f32[60,128]{1,0:T(8,128)S(1)} %get-tuple-element.56), channel_id=1, source_target_pairs={{0,224},{32,64},{64,32},{96,128},{128,96},{160,192},{192,160},{224... | collective-permute-start | bytes 92168 | tf_op jit(solution)/shard_map/ppermute | solution.py:534
  33.7 0.0 collective-permute-done.6.edges
  33.7 0.7 collective-permute-start.8
  34.4 0.0 collective-permute-done.2.be
  34.4 4.2 %collective-permute-done.3.bo = f32[10,64,128]{2,1,0:T(8,128)S(1)} collective-permute-done((f32[10,64,128]{2,1,0:T(8,128)S(1)}, f32[10,64,128]{2,1,0:T(8,128)S(1)}, u32[]{:S(2)}, u32[]{:S(2)}) %collective-permute-start.3) | collective-permute-done | bytes 327712 | tf_op jit(solution)/shard_map/ppermute | solution.py:534
  38.6 0.0 collective-permute-done.4.ce
  38.6 0.3 collective-permute-done.5.co
  38.9 1.9 %shard_map.40 = (f32[72,88,128]{2,1,0:T(8,128)S(1)}, f32[72,88,128]{2,1,0:T(8,128)S(1)}, f32[72,88,128]{2,1,0:T(8,128)S(1)}, f32[72,88,128]{2,1,0:T(8,128)S(1)},...) custom-call(f32[72,88,128]{2,1,0:T(8,128)S(1)} %get-tuple-element.42, ...), custom_call_target="tpu_custom_call", output_to_operand_aliasing={{0}: (0, {}), {1}: (1, {}), {2}: (2, {}), {3}: (3, {}), {4}... | custom-call | flops 100000000 | bytes 8000000 | tf_op jit(solution)/shard_map/pallas_call | solution.py:585
  40.9 0.1 collective-permute-start.12
  41.0 6.7 %collective-permute-start.13 = (f32[272,128]{1,0:T(8,128)S(1)}, f32[272,128]{1,0:T(8,128)S(1)}, u32[]{:S(2)}, u32[]{:S(2)}) collective-permute-start(f32[272,128]{1,0:T(8,128)S(1)} %get-tuple-element.65), channel_id=1, source_target_pairs={{0,31},{1,2},{2,1},{3,4},{4,3},{5,6},{6,5},{7,8},{8,7},{9,10},{10,... | collective-permute-start | bytes 417800 | tf_op jit(solution)/shard_map/ppermute | solution.py:534
  47.7 0.7 collective-permute-start.7
  48.4 0.0 collective-permute-done.8
  48.4 0.1 collective-permute-start.9
  48.5 0.0 collective-permute-done.12.le.re
  48.5 9.1 %collective-permute-done.13.lo.ro = f32[272,128]{1,0:T(8,128)S(1)} collective-permute-done((f32[272,128]{1,0:T(8,128)S(1)}, f32[272,128]{1,0:T(8,128)S(1)}, u32[]{:S(2)}, u32[]{:S(2)}) %collective-permute-start.13) | collective-permute-done | bytes 139296 | tf_op jit(solution)/shard_map/ppermute | solution.py:534
  57.6 0.1 shard_map.44
  57.7 0.5 collective-permute-start.14
  58.2 0.0 collective-permute-start.15
  58.2 0.0 collective-permute-done.7.near
  58.2 0.0 collective-permute-done.9.across
  58.2 0.1 shard_map.42
  58.3 0.2 collective-permute-start.10
  58.5 1.7 %collective-permute-start.11 = (f32[392,128]{1,0:T(8,128)S(1)}, f32[392,128]{1,0:T(8,128)S(1)}, u32[]{:S(2)}, u32[]{:S(2)}) collective-permute-start(f32[392,128]{1,0:T(8,128)S(1)} %get-tuple-element.63), channel_id=1, source_target_pairs={{0,224},{32,64},{64,32},{96,128},{128,96},{160,192},{192,160},{224... | collective-permute-start | bytes 602120 | tf_op jit(solution)/shard_map/ppermute | solution.py:534
  60.2 0.0 collective-permute-done.10.mbe
  60.2 10.3 %collective-permute-done.11.mbo = f32[392,128]{1,0:T(8,128)S(1)} collective-permute-done((f32[392,128]{1,0:T(8,128)S(1)}, f32[392,128]{1,0:T(8,128)S(1)}, u32[]{:S(2)}, u32[]{:S(2)}) %collective-permute-start.11) | collective-permute-done | bytes 200736 | tf_op jit(solution)/shard_map/ppermute | solution.py:534
  70.6 0.5 shard_map.43
  71.1 0.0 collective-permute-done.14.lbe
  71.1 0.0 collective-permute-done.15.lbo
  71.1 5.7 %shard_map.45 = (f32[64,64,128]{2,1,0:T(8,128)}, f32[72,88,128]{2,1,0:T(8,128)S(1)}) custom-call(f32[72,88,128]{2,1,0:T(8,128)S(1)} %get-tuple-element.66.v_in, f32[72,88,128]{2,1,0:T(8,128)S(1)} %get-tuple-element.67.f, f32[72,88,128]{2,1,0:T(8,128)S(1)} %get-tuple-element.68.w, ...), custom_call_target="tpu_custom_call", output_to_operand_aliasing={{1}: (0, {})} | custom-call | flops 100000000 | bytes 8000000 | tf_op jit(solution)/shard_map/pallas_call | solution.py:602
  (2 shorter events, 0.0 us)
Async XLA Ops:
  2.5 20.6 %collective-permute-start = (f32[640,128]{1,0:T(8,128)S(1)}, f32[640,128]{1,0:T(8,128)S(1)}, u32[]{:S(2)}, u32[]{:S(2)}) collective-permute-start(f32[640,128]{1,0:T(8,128)S(1)} %get-tuple-element.50), channel_id=1, source_target_pairs={{0,1},{1,0},{2,3},{3,2},{4,5},{5,4},{6,7},{7,6},{8,9},{9,8},{10,11... | collective-permute-start | bytes 983048 | tf_op jit(solution)/shard_map/ppermute | solution.py:529
  4.6 19.5 %collective-permute-start.1 = (f32[640,128]{1,0:T(8,128)S(1)}, f32[640,128]{1,0:T(8,128)S(1)}, u32[]{:S(2)}, u32[]{:S(2)}) collective-permute-start(f32[640,128]{1,0:T(8,128)S(1)} %get-tuple-element.51), channel_id=1, source_target_pairs={{0,31},{1,2},{2,1},{3,4},{4,3},{5,6},{6,5},{7,8},{8,7},{9,10},{10,... | collective-permute-start | bytes 983048 | tf_op jit(solution)/shard_map/ppermute | solution.py:534
  15.5 18.9 %collective-permute-start.2 = (f32[10,64,128]{2,1,0:T(8,128)S(1)}, f32[10,64,128]{2,1,0:T(8,128)S(1)}, u32[]{:S(2)}, u32[]{:S(2)}) collective-permute-start(f32[10,64,128]{2,1,0:T(8,128)S(1)} %get-tuple-element.52), channel_id=1, source_target_pairs={{0,32},{32,0},{64,96},{96,64},{128,160},{160,128},{192,224},{224,1... | collective-permute-start | bytes 983048 | tf_op jit(solution)/shard_map/ppermute | solution.py:529
  16.7 21.9 %collective-permute-start.3 = (f32[10,64,128]{2,1,0:T(8,128)S(1)}, f32[10,64,128]{2,1,0:T(8,128)S(1)}, u32[]{:S(2)}, u32[]{:S(2)}) collective-permute-start(f32[10,64,128]{2,1,0:T(8,128)S(1)} %get-tuple-element.53), channel_id=1, source_target_pairs={{0,224},{32,64},{64,32},{96,128},{128,96},{160,192},{192,160},{224... | collective-permute-start | bytes 983048 | tf_op jit(solution)/shard_map/ppermute | solution.py:534
  17.3 16.3 %collective-permute-start.6 = (f32[416,128]{1,0:T(8,128)S(1)}, f32[416,128]{1,0:T(8,128)S(1)}, u32[]{:S(2)}, u32[]{:S(2)}) collective-permute-start(f32[416,128]{1,0:T(8,128)S(1)} %get-tuple-element.59), channel_id=1, source_target_pairs={{0,1},{1,0},{2,3},{3,2},{4,5},{5,4},{6,7},{7,6},{8,9},{9,8},{10,11... | collective-permute-start | bytes 638984 | tf_op jit(solution)/shard_map/ppermute | solution.py:529
  24.1 14.5 %collective-permute-start.4 = (f32[60,128]{1,0:T(8,128)S(1)}, f32[60,128]{1,0:T(8,128)S(1)}, u32[]{:S(2)}, u32[]{:S(2)}) collective-permute-start(f32[60,128]{1,0:T(8,128)S(1)} %get-tuple-element.55), channel_id=1, source_target_pairs={{0,32},{32,0},{64,96},{96,64},{128,160},{160,128},{192,224},{224,1... | collective-permute-start | bytes 92168 | tf_op jit(solution)/shard_map/ppermute | solution.py:529
  31.8 7.1 %collective-permute-start.5 = (f32[60,128]{1,0:T(8,128)S(1)}, f32[60,128]{1,0:T(8,128)S(1)}, u32[]{:S(2)}, u32[]{:S(2)}) collective-permute-start(f32[60,128]{1,0:T(8,128)S(1)} %get-tuple-element.56), channel_id=1, source_target_pairs={{0,224},{32,64},{64,32},{96,128},{128,96},{160,192},{192,160},{224... | collective-permute-start | bytes 92168 | tf_op jit(solution)/shard_map/ppermute | solution.py:534
  33.7 14.7 %collective-permute-start.8 = (f32[208,128]{1,0:T(8,128)S(1)}, f32[208,128]{1,0:T(8,128)S(1)}, u32[]{:S(2)}, u32[]{:S(2)}) collective-permute-start(f32[208,128]{1,0:T(8,128)S(1)} %shard_map.41), channel_id=1, source_target_pairs={{14,17},{30,1},{17,14},{1,30},{46,49},{62,33},{49,46},{33,62},{78,... | collective-permute-start | bytes 319496 | tf_op jit(solution)/shard_map/ppermute | solution.py:566
  40.9 7.6 %collective-permute-start.12 = (f32[272,128]{1,0:T(8,128)S(1)}, f32[272,128]{1,0:T(8,128)S(1)}, u32[]{:S(2)}, u32[]{:S(2)}) collective-permute-start(f32[272,128]{1,0:T(8,128)S(1)} %get-tuple-element.64), channel_id=1, source_target_pairs={{0,1},{1,0},{2,3},{3,2},{4,5},{5,4},{6,7},{7,6},{8,9},{9,8},{10,11... | collective-permute-start | bytes 417800 | tf_op jit(solution)/shard_map/ppermute | solution.py:529
  41.0 16.7 %collective-permute-start.13 = (f32[272,128]{1,0:T(8,128)S(1)}, f32[272,128]{1,0:T(8,128)S(1)}, u32[]{:S(2)}, u32[]{:S(2)}) collective-permute-start(f32[272,128]{1,0:T(8,128)S(1)} %get-tuple-element.65), channel_id=1, source_target_pairs={{0,31},{1,2},{2,1},{3,4},{4,3},{5,6},{6,5},{7,8},{8,7},{9,10},{10,... | collective-permute-start | bytes 417800 | tf_op jit(solution)/shard_map/ppermute | solution.py:534
  47.7 10.5 %collective-permute-start.7 = (f32[208,128]{1,0:T(8,128)S(1)}, f32[208,128]{1,0:T(8,128)S(1)}, u32[]{:S(2)}, u32[]{:S(2)}) collective-permute-start(f32[208,128]{1,0:T(8,128)S(1)} %get-tuple-element.60), channel_id=1, source_target_pairs={{1,2},{3,4},{5,6},{7,8},{9,10},{11,12},{13,14},{17,18},{19,20},{21... | collective-permute-start | bytes 319496 | tf_op jit(solution)/shard_map/ppermute | solution.py:563
  48.4 9.8 %collective-permute-start.9 = (f32[208,128]{1,0:T(8,128)S(1)}, f32[208,128]{1,0:T(8,128)S(1)}, u32[]{:S(2)}, u32[]{:S(2)}) collective-permute-start(f32[208,128]{1,0:T(8,128)S(1)} %collective-permute-done.8), channel_id=1, source_target_pairs={{0,1},{1,0},{2,3},{3,2},{4,5},{5,4},{6,7},{7,6},{8,9},{9,8},{10,11... | collective-permute-start | bytes 319496 | tf_op jit(solution)/shard_map/ppermute | solution.py:529
  57.7 13.4 %collective-permute-start.14 = (f32[464,128]{1,0:T(8,128)S(1)}, f32[464,128]{1,0:T(8,128)S(1)}, u32[]{:S(2)}, u32[]{:S(2)}) collective-permute-start(f32[464,128]{1,0:T(8,128)S(1)} %get-tuple-element.74), channel_id=1, source_target_pairs={{0,32},{32,0},{64,96},{96,64},{128,160},{160,128},{192,224},{224,1... | collective-permute-start | bytes 712712 | tf_op jit(solution)/shard_map/ppermute | solution.py:529
  58.2 12.9 %collective-permute-start.15 = (f32[464,128]{1,0:T(8,128)S(1)}, f32[464,128]{1,0:T(8,128)S(1)}, u32[]{:S(2)}, u32[]{:S(2)}) collective-permute-start(f32[464,128]{1,0:T(8,128)S(1)} %get-tuple-element.75), channel_id=1, source_target_pairs={{0,224},{32,64},{64,32},{96,128},{128,96},{160,192},{192,160},{224... | collective-permute-start | bytes 712712 | tf_op jit(solution)/shard_map/ppermute | solution.py:534
  58.3 1.9 %collective-permute-start.10 = (f32[392,128]{1,0:T(8,128)S(1)}, f32[392,128]{1,0:T(8,128)S(1)}, u32[]{:S(2)}, u32[]{:S(2)}) collective-permute-start(f32[392,128]{1,0:T(8,128)S(1)} %get-tuple-element.62), channel_id=1, source_target_pairs={{0,32},{32,0},{64,96},{96,64},{128,160},{160,128},{192,224},{224,1... | collective-permute-start | bytes 602120 | tf_op jit(solution)/shard_map/ppermute | solution.py:529
  58.5 12.1 %collective-permute-start.11 = (f32[392,128]{1,0:T(8,128)S(1)}, f32[392,128]{1,0:T(8,128)S(1)}, u32[]{:S(2)}, u32[]{:S(2)}) collective-permute-start(f32[392,128]{1,0:T(8,128)S(1)} %get-tuple-element.63), channel_id=1, source_target_pairs={{0,224},{32,64},{64,32},{96,128},{128,96},{160,192},{192,160},{224... | collective-permute-start | bytes 602120 | tf_op jit(solution)/shard_map/ppermute | solution.py:534

commit v2 on v1

--- a/solution.py
+++ b/solution.py
@@ -32,7 +32,10 @@
 WIDTHS = [C + 2 * (H + 1 - j) for j in range(1, H + 1)]
 STARTS = [sum(WIDTHS[:k]) for k in range(H)]
 BAND_COARSE = -(-sum(WIDTHS) // 8) * 8
+BAND_OWN = C * H
 BAND_RIM = N + 8
+BAND_LATE = -(-H * (H + 1) // 8) * 8
+REACHES = [(j, H + 1 - j, (j - 1) * (2 * H + 2) - (j - 1) * j) for j in range(1, H + 1)]
 LANE_COARSE = C * H
 PIECES = 4
 FIT = 16 * 2**20
@@ -224,6 +227,22 @@
         ext[CR0 + C + j - 1, cols, :] = below[at : at + wide, :]
 
 
+def pack_late(ext, down, up):
+    for j, reach, at in REACHES:
+        for dst, row in ((down, CR0 + C - j), (up, CR0 + j - 1)):
+            dst[at : at + reach, :] = ext[row, CC0 - reach : CC0, :]
+            dst[at + reach : at + 2 * reach, :] = ext[row, CC0 + C : CC0 + C + reach, :]
+    for dst in (down, up):
+        dst[H * (H + 1) :, :] = jnp.zeros((BAND_LATE - H * (H + 1), L), f32)
+
+
+def place_late(ext, above, below):
+    for j, reach, at in REACHES:
+        for msg, row in ((above, CR0 - j), (below, CR0 + C + j - 1)):
+            ext[row, CC0 - reach : CC0, :] = msg[at : at + reach, :]
+            ext[row, CC0 + C : CC0 + C + reach, :] = msg[at + reach : at + 2 * reach, :]
+
+
 def weight(mass):
     return 0.8 / (4.0 + mass)
 
@@ -377,8 +396,11 @@
     either(lane_even, lambda: out_lanes(l_even, l_odd), lambda: out_lanes(l_odd, l_even))
 
     def out_bands(down, up):
+        for j in range(1, H + 1):
+            down[(j - 1) * C : j * C, :] = cl[C - j]
+            up[(j - 1) * C : j * C, :] = cl[j - 1]
         for dst, rim, edge in ((down, R1 - 2, R1 - 1), (up, R0 + 1, R0)):
-            at = 0
+            at = BAND_OWN
             dst[at : at + N, :] = v3[rim, C0:C1, :]
             dst[at + N : at + N + 8, :] = jnp.zeros((8, L), f32)
             dst[at + N : at + N + 1, :] = v3[edge, C0 - 1 : C0, :]
@@ -418,7 +440,7 @@
     )
 
 
-def coarse_bands(cl, re, ro, rim_even, rim_odd, lext, b_even, b_odd):
+def coarse_bands(cl, re, ro, lext, b_even, b_odd):
     for i in range(C):
         lext[CR0 + i, CC0 : CC0 + C, :] = cl[i]
     either(
@@ -428,15 +450,13 @@
     )
     either(
         parity("band"),
-        lambda: pack_coarse_bands(lext, b_even, b_odd),
-        lambda: pack_coarse_bands(lext, b_odd, b_even),
+        lambda: pack_late(lext, b_even, b_odd),
+        lambda: pack_late(lext, b_odd, b_even),
     )
-    b_even[BAND_COARSE:, :] = rim_even[...]
-    b_odd[BAND_COARSE:, :] = rim_odd[...]
-
-
-def between(v_in, mext, mbe, mbo, le, lo, v, wext, ext):
-    del v_in
+
+
+def between(v_in, lext_in, mext, mbe, mbo, le, lo, rbe, rbo, v, lext, wext, ext):
+    del v_in, lext_in
 
     def lanes(left, right):
         def group(g, carry):
@@ -454,32 +474,36 @@
     for i in range(C):
         ext[CR0 + i, span, :] = mext[CR0 + i, span, :]
 
-    def bands(above, below):
-        place_coarse_bands(ext, above, below)
-
-    either(parity("band"), lambda: bands(mbo, mbe), lambda: bands(mbe, mbo))
-
-    def weights(r):
-        wext[r] = weight(ext[r])
-
-    loop(CR, 2, weights)
-
-
-def after(v_in, f, w, wext, lext_in, lbe, lbo, result, v, lext, a, b, wide, t, s, out, sems):
-    span = slice(CC0 - H, CC0 + C + H)
-    for i in range(C):
-        lext[CR0 + i, span, :] = lext_in[CR0 + i, span, :]
-    del v_in
-
-    def bands(above, below):
-        place_coarse_bands(lext, above, below)
+    def own(above, below):
+        for j in range(1, H + 1):
+            lext[CR0 - j, CC0 : CC0 + C, :] = above[(j - 1) * C : j * C, :]
+            lext[CR0 + C + j - 1, CC0 : CC0 + C, :] = below[(j - 1) * C : j * C, :]
         for msg, rim, edge in ((above, R0 - 2, R0 - 1), (below, R1 + 1, R1)):
-            at = BAND_COARSE
+            at = BAND_OWN
             v[rim, C0:C1, :] = msg[at : at + N, :]
             v[edge, C0 - 1 : C0, :] = msg[at + N : at + N + 1, :]
             v[edge, C1 : C1 + 1, :] = msg[at + N + 1 : at + N + 2, :]
 
-    either(parity("band"), lambda: bands(lbo, lbe), lambda: bands(lbe, lbo))
+    either(parity("band"), lambda: own(rbo, rbe), lambda: own(rbe, rbo))
+
+    def bands(above, below):
+        place_coarse_bands(ext, above, below)
+
+    either(parity("band"), lambda: bands(mbo, mbe), lambda: bands(mbe, mbo))
+
+    def weights(r):
+        wext[r] = weight(ext[r])
+
+    loop(CR, 2, weights)
+
+
+def after(v, f, w, wext, lext_in, lbe, lbo, result, lext, a, b, wide, t, s, out, sems):
+    del lext_in
+    either(
+        parity("band"),
+        lambda: place_late(lext, lbo, lbe),
+        lambda: place_late(lext, lbe, lbo),
+    )
 
     def first(r):
         a[r] = wext[r] * lext[r]
@@ -540,9 +564,9 @@
     own, fine = sds(N, N, L), sds(ROWS, COLS, L)
     corner = sds(2 * DF * DEPTH, L)
     lane_msg, band_msg = sds(FINE, L), sds(DEPTH, N, L)
-    rim, lane_mass = sds(BAND_RIM, L), sds(LANE_COARSE, L)
+    early, lane_mass = sds(BAND_OWN + BAND_RIM, L), sds(LANE_COARSE, L)
     lane_coarse, band_coarse = sds(LANE_COARSE + N, L), sds(BAND_COARSE, L)
-    band_both = sds(BAND_COARSE + BAND_RIM, L)
+    band_late = sds(BAND_LATE, L)
     coarse, own_coarse = sds(CR, CCOLS, L), sds(C, C, L)
     coarse_buf, fine_buf = pltpu.VMEM((CR, CCOLS, L), f32), pltpu.VMEM((ROWS, COLS, L), f32)
     own_buf, line = pltpu.VMEM((N, N, L), f32), pltpu.VMEM((N, L), f32)
@@ -584,28 +608,27 @@
 
     u, f, w, v1, v2, v3, cl, le, lo, rime, rimo = call(
         before,
-        [fine] * 6 + [own_coarse, lane_coarse, lane_coarse, rim, rim],
+        [fine] * 6 + [own_coarse, lane_coarse, lane_coarse, early, early],
         [VM] * 14,
         [pltpu.VMEM((N * DF, L), f32), pltpu.VMEM((N * DF, L), f32), pltpu.VMEM(corner.shape, f32), line],
         aliases={k: k for k in range(7)},
         flops=10**8,
     )(u, f, w, v1, v2, v3, cl, a4, re, ro, rbe, rbo, rce, rco)
     rlo, rle = swap_odd(lo, "lane"), swap_even(le, "lane")
-    lext, lbe, lbo = call(
-        coarse_bands, [coarse, band_both, band_both], [VM] * 5
-    )(cl, rle, rlo, rime, rimo)
+    rrimo, rrime = swap_odd(rimo, "band"), swap_even(rime, "band")
+    lext, lbe, lbo = call(coarse_bands, [coarse, band_late, band_late], [VM] * 3)(cl, rle, rlo)
     rlbo, rlbe = swap_odd(lbo, "band"), swap_even(lbe, "band")
-    v3, wext = call(
-        between, [fine, coarse], [VM] * 6, [coarse_buf], aliases={0: 0}, flops=10**7
-    )(v3, mext, rmbe, rmbo, rle, rlo)
+    v3, lext, wext = call(
+        between, [fine, coarse, coarse], [VM] * 9, [coarse_buf], aliases={0: 0, 1: 1}, flops=10**7
+    )(v3, lext, mext, rmbe, rmbo, rle, rlo, rrime, rrimo)
 
     out, _ = call(
         after,
-        [own, fine],
+        [own, coarse],
         [VM] * 7,
-        [coarse_buf] * 3 + [pltpu.VMEM((N + 8, L), f32), fine_buf, fine_buf, own_buf, dma((PIECES,))],
+        [coarse_buf] * 2 + [pltpu.VMEM((N + 8, L), f32), fine_buf, fine_buf, own_buf, dma((PIECES,))],
         flops=10**8,
-        aliases={0: 1},
+        aliases={4: 1},
         result=True,
     )(v3, f, w, wext, lext, rlbe, rlbo)
     return out

time: 76.9 us -> 71.9 us (0.935)
  waiting for transfers between devices: 25.1 us -> 18.2 us
  starting transfers between devices: 35.1 us -> 36.8 us
    ppermute x6 -> x7, waiting for transfers between devices: 25.1 us -> 12 us  [swap_odd(): lax.ppermute(x, axis, [(i, (i + 1) % n if i % 2 else (i - 1) % n) for i i...]
    ppermute x8 -> x9, waiting for transfers between devices: 0.02 us -> 6.2 us  [swap_even(): return lax.ppermute(x, axis, [(i, i ^ 1) for i in range(n)])]
    ppermute x8 -> x9, starting transfers between devices: 12 us -> 16.3 us  [swap_even(): return lax.ppermute(x, axis, [(i, i ^ 1) for i in range(n)])]
    ppermute x6 -> x7, starting transfers between devices: 21.8 us -> 19.1 us  [swap_odd(): lax.ppermute(x, axis, [(i, (i + 1) % n if i % 2 else (i - 1) % n) for i i...]
  transfers between devices with their start and end apart: 16 -> 18, of which waited for: 5 -> 4; matrix products, arithmetic and copies ran while one was open for 0% -> 0% of each run, Pallas kernels for 11% -> 12%
where the time goes in v2:
time: 71.9 us; the launch traced here: 71.8 us
  starting transfers between devices  36.8 us (51%)
  waiting for transfers between devices  18.2 us (25%)
  Pallas kernels  16.7 us (23%)
    ppermute x7, starting transfers between devices, swap_odd(): lax.ppermute(x, axis, [(i, (i + 1) % n if i % 2 else (i - 1) % n) for i i...  19.1 us
    ppermute x9, starting transfers between devices, swap_even(): return lax.ppermute(x, axis, [(i, i ^ 1) for i in range(n)])  16.3 us
    ppermute x7, waiting for transfers between devices, swap_odd(): lax.ppermute(x, axis, [(i, (i + 1) % n if i % 2 else (i - 1) % n) for i i...  12 us
    ppermute x9, waiting for transfers between devices, swap_even(): return lax.ppermute(x, axis, [(i, i ^ 1) for i in range(n)])  6.2 us
    pallas_call x1, Pallas kernels, shards(): call(prepare, [fine] * 7 + [own_coarse, sds(8, L)], [HBM, HBM, VM], [own_...  6.13 us
    pallas_call x1, Pallas kernels, shards(): call(after, [own, coarse], [VM] * 7, [coarse_buf] * 2 + [pltpu.VMEM((N +...  5.33 us
    pallas_call x1, Pallas kernels, shards(): call(pack_fine, [lane_msg, lane_msg, band_msg, band_msg, own, own_coarse,...  2.47 us
    pallas_call x1, Pallas kernels, shards(): call(before, [fine] * 6 + [own_coarse, lane_coarse, lane_coarse, early, e...  2 us
  transfers between devices with their start and end apart: 18, of which 4 were waited for; matrix products, arithmetic and copies ran while one was open for 0% of the time, Pallas kernels for 12%

profile of v2, /device:TPU:1, one launch (start us, length us, event | category | flops | bytes accessed | tf_op | source)
XLA Modules:
  0.0 71.8 jit_solution(11697581000510614243)
XLA Ops:
  0.0 2.5 %shard_map.37 = (f32[640,128]{1,0:T(8,128)S(1)}, f32[640,128]{1,0:T(8,128)S(1)}, f32[10,64,128]{2,1,0:T(8,128)S(1)}, f32[10,64,128]{2,1,0:T(8,128)S(1)}, f32[64,...) custom-call(f32[64,64,128]{2,1,0:T(8,128)} %load.3, ...), custom_call_target="tpu_custom_call" | custom-call | flops 1000000 | bytes 8000000 | tf_op jit(solution)/shard_map/pallas_call | solution.py:574
  2.5 2.1 %collective-permute-start = (f32[640,128]{1,0:T(8,128)S(1)}, f32[640,128]{1,0:T(8,128)S(1)}, u32[]{:S(2)}, u32[]{:S(2)}) collective-permute-start(f32[640,128]{1,0:T(8,128)S(1)} %get-tuple-element.51), channel_id=1, source_target_pairs={{0,1},{1,0},{2,3},{3,2},{4,5},{5,4},{6,7},{7,6},{8,9},{9,8},{10,11... | collective-permute-start | bytes 983048 | tf_op jit(solution)/shard_map/ppermute | solution.py:553
  4.6 10.9 %collective-permute-start.1 = (f32[640,128]{1,0:T(8,128)S(1)}, f32[640,128]{1,0:T(8,128)S(1)}, u32[]{:S(2)}, u32[]{:S(2)}) collective-permute-start(f32[640,128]{1,0:T(8,128)S(1)} %get-tuple-element.52), channel_id=1, source_target_pairs={{0,31},{1,2},{2,1},{3,4},{4,3},{5,6},{6,5},{7,8},{8,7},{9,10},{10,... | collective-permute-start | bytes 983048 | tf_op jit(solution)/shard_map/ppermute | solution.py:558
  15.5 1.2 %collective-permute-start.2 = (f32[10,64,128]{2,1,0:T(8,128)S(1)}, f32[10,64,128]{2,1,0:T(8,128)S(1)}, u32[]{:S(2)}, u32[]{:S(2)}) collective-permute-start(f32[10,64,128]{2,1,0:T(8,128)S(1)} %get-tuple-element.53), channel_id=1, source_target_pairs={{0,32},{32,0},{64,96},{96,64},{128,160},{160,128},{192,224},{224,1... | collective-permute-start | bytes 983048 | tf_op jit(solution)/shard_map/ppermute | solution.py:553
  16.7 0.0 collective-permute-start.8
  16.7 0.6 collective-permute-start.3
  17.4 6.2 %collective-permute-done.8.edges = f32[416,128]{1,0:T(8,128)S(1)} collective-permute-done((f32[416,128]{1,0:T(8,128)S(1)}, f32[416,128]{1,0:T(8,128)S(1)}, u32[]{:S(2)}, u32[]{:S(2)}) %collective-permute-start.8) | collective-permute-done | bytes 213024 | tf_op jit(solution)/shard_map/ppermute | solution.py:553
  23.5 0.7 collective-permute-start.10
  24.2 6.1 %shard_map.38 = (f32[72,88,128]{2,1,0:T(8,128)S(1)}, f32[72,88,128]{2,1,0:T(8,128)S(1)}, f32[72,88,128]{2,1,0:T(8,128)S(1)}, f32[72,88,128]{2,1,0:T(8,128)S(1)},...) custom-call(f32[64,64,128]{2,1,0:T(8,128)} %load.3, ...), custom_call_target="tpu_custom_call" | custom-call | flops 100000000 | bytes 8000000 | tf_op jit(solution)/shard_map/pallas_call | solution.py:593
  30.4 0.0 collective-permute-done.m_even.re
  30.4 0.0 collective-permute-done.1.m_odd.ro
  30.4 1.4 %collective-permute-start.4 = (f32[60,128]{1,0:T(8,128)S(1)}, f32[60,128]{1,0:T(8,128)S(1)}, u32[]{:S(2)}, u32[]{:S(2)}) collective-permute-start(f32[60,128]{1,0:T(8,128)S(1)} %get-tuple-element.56), channel_id=1, source_target_pairs={{0,32},{32,0},{64,96},{96,64},{128,160},{160,128},{192,224},{224,1... | collective-permute-start | bytes 92168 | tf_op jit(solution)/shard_map/ppermute | solution.py:553
  31.8 1.8 %collective-permute-start.5 = (f32[60,128]{1,0:T(8,128)S(1)}, f32[60,128]{1,0:T(8,128)S(1)}, u32[]{:S(2)}, u32[]{:S(2)}) collective-permute-start(f32[60,128]{1,0:T(8,128)S(1)} %get-tuple-element.57), channel_id=1, source_target_pairs={{0,224},{32,64},{64,32},{96,128},{128,96},{160,192},{192,160},{224... | collective-permute-start | bytes 92168 | tf_op jit(solution)/shard_map/ppermute | solution.py:558
  33.6 0.0 collective-permute-done.10
  33.6 0.7 collective-permute-start.9
  34.3 0.0 collective-permute-done.2.be
  34.3 6.5 %collective-permute-start.11 = (f32[208,128]{1,0:T(8,128)S(1)}, f32[208,128]{1,0:T(8,128)S(1)}, u32[]{:S(2)}, u32[]{:S(2)}) collective-permute-start(f32[208,128]{1,0:T(8,128)S(1)} %collective-permute-done.10), channel_id=1, source_target_pairs={{0,1},{1,0},{2,3},{3,2},{4,5},{5,4},{6,7},{7,6},{8,9},{9,8},{10,11... | collective-permute-start | bytes 319496 | tf_op jit(solution)/shard_map/ppermute | solution.py:553
  40.8 0.0 collective-permute-done.3.bo
  40.8 0.0 collective-permute-done.4.ce
  40.8 0.0 collective-permute-done.5.co
  40.8 2.0 %shard_map.40 = (f32[72,88,128]{2,1,0:T(8,128)S(1)}, f32[72,88,128]{2,1,0:T(8,128)S(1)}, f32[72,88,128]{2,1,0:T(8,128)S(1)}, f32[72,88,128]{2,1,0:T(8,128)S(1)},...) custom-call(f32[72,88,128]{2,1,0:T(8,128)S(1)} %get-tuple-element.43, ...), custom_call_target="tpu_custom_call", output_to_operand_aliasing={{0}: (0, {}), {1}: (1, {}), {2}: (2, {}), {3}: (3, {}), {4}... | custom-call | flops 100000000 | bytes 8000000 | tf_op jit(solution)/shard_map/pallas_call | solution.py:609
  42.8 0.6 collective-permute-start.6
  43.5 2.2 %collective-permute-start.14 = (f32[280,128]{1,0:T(8,128)S(1)}, f32[280,128]{1,0:T(8,128)S(1)}, u32[]{:S(2)}, u32[]{:S(2)}) collective-permute-start(f32[280,128]{1,0:T(8,128)S(1)} %get-tuple-element.69), channel_id=1, source_target_pairs={{0,32},{32,0},{64,96},{96,64},{128,160},{160,128},{192,224},{224,1... | collective-permute-start | bytes 430088 | tf_op jit(solution)/shard_map/ppermute | solution.py:553
  45.7 4.0 %collective-permute-start.7 = (f32[272,128]{1,0:T(8,128)S(1)}, f32[272,128]{1,0:T(8,128)S(1)}, u32[]{:S(2)}, u32[]{:S(2)}) collective-permute-start(f32[272,128]{1,0:T(8,128)S(1)} %get-tuple-element.61), channel_id=1, source_target_pairs={{0,31},{1,2},{2,1},{3,4},{4,3},{5,6},{6,5},{7,8},{8,7},{9,10},{10,... | collective-permute-start | bytes 417800 | tf_op jit(solution)/shard_map/ppermute | solution.py:558
  49.7 0.0 collective-permute-done.9.near
  49.7 0.0 collective-permute-done.11.across
  49.7 0.1 shard_map.43
  49.8 0.5 collective-permute-start.12
  50.2 1.5 %collective-permute-start.13 = (f32[392,128]{1,0:T(8,128)S(1)}, f32[392,128]{1,0:T(8,128)S(1)}, u32[]{:S(2)}, u32[]{:S(2)}) collective-permute-start(f32[392,128]{1,0:T(8,128)S(1)} %get-tuple-element.68), channel_id=1, source_target_pairs={{0,224},{32,64},{64,32},{96,128},{128,96},{160,192},{192,160},{224... | collective-permute-start | bytes 602120 | tf_op jit(solution)/shard_map/ppermute | solution.py:558
  51.7 0.0 collective-permute-done.6.re.le
  51.7 0.3 collective-permute-start.15
  52.0 8.7 %collective-permute-done.7.ro.lo = f32[272,128]{1,0:T(8,128)S(1)} collective-permute-done((f32[272,128]{1,0:T(8,128)S(1)}, f32[272,128]{1,0:T(8,128)S(1)}, u32[]{:S(2)}, u32[]{:S(2)}) %collective-permute-start.7) | collective-permute-done | bytes 139296 | tf_op jit(solution)/shard_map/ppermute | solution.py:558
  60.7 0.1 shard_map.41
  60.8 1.7 %collective-permute-start.16 = (f32[184,128]{1,0:T(8,128)S(1)}, f32[184,128]{1,0:T(8,128)S(1)}, u32[]{:S(2)}, u32[]{:S(2)}) collective-permute-start(f32[184,128]{1,0:T(8,128)S(1)} %get-tuple-element.76), channel_id=1, source_target_pairs={{0,32},{32,0},{64,96},{96,64},{128,160},{160,128},{192,224},{224,1... | collective-permute-start | bytes 282632 | tf_op jit(solution)/shard_map/ppermute | solution.py:553
  62.5 0.0 collective-permute-done.14.rbe
  62.5 0.1 collective-permute-start.17
  62.6 2.9 %collective-permute-done.15.rbo = f32[280,128]{1,0:T(8,128)S(1)} collective-permute-done((f32[280,128]{1,0:T(8,128)S(1)}, f32[280,128]{1,0:T(8,128)S(1)}, u32[]{:S(2)}, u32[]{:S(2)}) %collective-permute-start.15) | collective-permute-done | bytes 143392 | tf_op jit(solution)/shard_map/ppermute | solution.py:558
  65.5 0.0 collective-permute-done.12.mbe
  65.5 0.0 collective-permute-done.13.mbo
  65.5 0.5 shard_map.44
  66.0 0.0 collective-permute-done.16.lbe
  66.0 0.4 collective-permute-done.17.lbo
  66.5 5.3 %shard_map.45 = (f32[64,64,128]{2,1,0:T(8,128)}, f32[42,56,128]{2,1,0:T(8,128)S(1)}) custom-call(f32[72,88,128]{2,1,0:T(8,128)S(1)} %get-tuple-element.71.v, f32[72,88,128]{2,1,0:T(8,128)S(1)} %get-tuple-element.72.f, f32[72,88,128]{2,1,0:T(8,128)S(1)} %get-tuple-element.73.w, ...), custom_call_target="tpu_custom_call", output_to_operand_aliasing={{1}: (4, {})} | custom-call | flops 100000000 | bytes 8000000 | tf_op jit(solution)/shard_map/pallas_call | solution.py:625
  (2 shorter events, 0.0 us)
Async XLA Ops:
  2.5 27.9 %collective-permute-start = (f32[640,128]{1,0:T(8,128)S(1)}, f32[640,128]{1,0:T(8,128)S(1)}, u32[]{:S(2)}, u32[]{:S(2)}) collective-permute-start(f32[640,128]{1,0:T(8,128)S(1)} %get-tuple-element.51), channel_id=1, source_target_pairs={{0,1},{1,0},{2,3},{3,2},{4,5},{5,4},{6,7},{7,6},{8,9},{9,8},{10,11... | collective-permute-start | bytes 983048 | tf_op jit(solution)/shard_map/ppermute | solution.py:553
  4.6 25.8 %collective-permute-start.1 = (f32[640,128]{1,0:T(8,128)S(1)}, f32[640,128]{1,0:T(8,128)S(1)}, u32[]{:S(2)}, u32[]{:S(2)}) collective-permute-start(f32[640,128]{1,0:T(8,128)S(1)} %get-tuple-element.52), channel_id=1, source_target_pairs={{0,31},{1,2},{2,1},{3,4},{4,3},{5,6},{6,5},{7,8},{8,7},{9,10},{10,... | collective-permute-start | bytes 983048 | tf_op jit(solution)/shard_map/ppermute | solution.py:558
  15.5 18.8 %collective-permute-start.2 = (f32[10,64,128]{2,1,0:T(8,128)S(1)}, f32[10,64,128]{2,1,0:T(8,128)S(1)}, u32[]{:S(2)}, u32[]{:S(2)}) collective-permute-start(f32[10,64,128]{2,1,0:T(8,128)S(1)} %get-tuple-element.53), channel_id=1, source_target_pairs={{0,32},{32,0},{64,96},{96,64},{128,160},{160,128},{192,224},{224,1... | collective-permute-start | bytes 983048 | tf_op jit(solution)/shard_map/ppermute | solution.py:553
  16.7 6.8 %collective-permute-start.8 = (f32[416,128]{1,0:T(8,128)S(1)}, f32[416,128]{1,0:T(8,128)S(1)}, u32[]{:S(2)}, u32[]{:S(2)}) collective-permute-start(f32[416,128]{1,0:T(8,128)S(1)} %get-tuple-element.64), channel_id=1, source_target_pairs={{0,1},{1,0},{2,3},{3,2},{4,5},{5,4},{6,7},{7,6},{8,9},{9,8},{10,11... | collective-permute-start | bytes 638984 | tf_op jit(solution)/shard_map/ppermute | solution.py:553
  16.7 24.1 %collective-permute-start.3 = (f32[10,64,128]{2,1,0:T(8,128)S(1)}, f32[10,64,128]{2,1,0:T(8,128)S(1)}, u32[]{:S(2)}, u32[]{:S(2)}) collective-permute-start(f32[10,64,128]{2,1,0:T(8,128)S(1)} %get-tuple-element.54), channel_id=1, source_target_pairs={{0,224},{32,64},{64,32},{96,128},{128,96},{160,192},{192,160},{224... | collective-permute-start | bytes 983048 | tf_op jit(solution)/shard_map/ppermute | solution.py:558
  23.5 10.1 %collective-permute-start.10 = (f32[208,128]{1,0:T(8,128)S(1)}, f32[208,128]{1,0:T(8,128)S(1)}, u32[]{:S(2)}, u32[]{:S(2)}) collective-permute-start(f32[208,128]{1,0:T(8,128)S(1)} %shard_map.42), channel_id=1, source_target_pairs={{14,17},{30,1},{17,14},{1,30},{46,49},{62,33},{49,46},{33,62},{78,... | collective-permute-start | bytes 319496 | tf_op jit(solution)/shard_map/ppermute | solution.py:590
  30.4 10.4 %collective-permute-start.4 = (f32[60,128]{1,0:T(8,128)S(1)}, f32[60,128]{1,0:T(8,128)S(1)}, u32[]{:S(2)}, u32[]{:S(2)}) collective-permute-start(f32[60,128]{1,0:T(8,128)S(1)} %get-tuple-element.56), channel_id=1, source_target_pairs={{0,32},{32,0},{64,96},{96,64},{128,160},{160,128},{192,224},{224,1... | collective-permute-start | bytes 92168 | tf_op jit(solution)/shard_map/ppermute | solution.py:553
  31.8 9.0 %collective-permute-start.5 = (f32[60,128]{1,0:T(8,128)S(1)}, f32[60,128]{1,0:T(8,128)S(1)}, u32[]{:S(2)}, u32[]{:S(2)}) collective-permute-start(f32[60,128]{1,0:T(8,128)S(1)} %get-tuple-element.57), channel_id=1, source_target_pairs={{0,224},{32,64},{64,32},{96,128},{128,96},{160,192},{192,160},{224... | collective-permute-start | bytes 92168 | tf_op jit(solution)/shard_map/ppermute | solution.py:558
  33.6 16.0 %collective-permute-start.9 = (f32[208,128]{1,0:T(8,128)S(1)}, f32[208,128]{1,0:T(8,128)S(1)}, u32[]{:S(2)}, u32[]{:S(2)}) collective-permute-start(f32[208,128]{1,0:T(8,128)S(1)} %get-tuple-element.65), channel_id=1, source_target_pairs={{1,2},{3,4},{5,6},{7,8},{9,10},{11,12},{13,14},{17,18},{19,20},{21... | collective-permute-start | bytes 319496 | tf_op jit(solution)/shard_map/ppermute | solution.py:587
  34.3 15.4 %collective-permute-start.11 = (f32[208,128]{1,0:T(8,128)S(1)}, f32[208,128]{1,0:T(8,128)S(1)}, u32[]{:S(2)}, u32[]{:S(2)}) collective-permute-start(f32[208,128]{1,0:T(8,128)S(1)} %collective-permute-done.10), channel_id=1, source_target_pairs={{0,1},{1,0},{2,3},{3,2},{4,5},{5,4},{6,7},{7,6},{8,9},{9,8},{10,11... | collective-permute-start | bytes 319496 | tf_op jit(solution)/shard_map/ppermute | solution.py:553
  42.8 8.9 %collective-permute-start.6 = (f32[272,128]{1,0:T(8,128)S(1)}, f32[272,128]{1,0:T(8,128)S(1)}, u32[]{:S(2)}, u32[]{:S(2)}) collective-permute-start(f32[272,128]{1,0:T(8,128)S(1)} %get-tuple-element.60), channel_id=1, source_target_pairs={{0,1},{1,0},{2,3},{3,2},{4,5},{5,4},{6,7},{7,6},{8,9},{9,8},{10,11... | collective-permute-start | bytes 417800 | tf_op jit(solution)/shard_map/ppermute | solution.py:553
  43.5 19.0 %collective-permute-start.14 = (f32[280,128]{1,0:T(8,128)S(1)}, f32[280,128]{1,0:T(8,128)S(1)}, u32[]{:S(2)}, u32[]{:S(2)}) collective-permute-start(f32[280,128]{1,0:T(8,128)S(1)} %get-tuple-element.69), channel_id=1, source_target_pairs={{0,32},{32,0},{64,96},{96,64},{128,160},{160,128},{192,224},{224,1... | collective-permute-start | bytes 430088 | tf_op jit(solution)/shard_map/ppermute | solution.py:553
  45.7 15.0 %collective-permute-start.7 = (f32[272,128]{1,0:T(8,128)S(1)}, f32[272,128]{1,0:T(8,128)S(1)}, u32[]{:S(2)}, u32[]{:S(2)}) collective-permute-start(f32[272,128]{1,0:T(8,128)S(1)} %get-tuple-element.61), channel_id=1, source_target_pairs={{0,31},{1,2},{2,1},{3,4},{4,3},{5,6},{6,5},{7,8},{8,7},{9,10},{10,... | collective-permute-start | bytes 417800 | tf_op jit(solution)/shard_map/ppermute | solution.py:558
  49.8 15.7 %collective-permute-start.12 = (f32[392,128]{1,0:T(8,128)S(1)}, f32[392,128]{1,0:T(8,128)S(1)}, u32[]{:S(2)}, u32[]{:S(2)}) collective-permute-start(f32[392,128]{1,0:T(8,128)S(1)} %get-tuple-element.67), channel_id=1, source_target_pairs={{0,32},{32,0},{64,96},{96,64},{128,160},{160,128},{192,224},{224,1... | collective-permute-start | bytes 602120 | tf_op jit(solution)/shard_map/ppermute | solution.py:553
  50.2 15.2 %collective-permute-start.13 = (f32[392,128]{1,0:T(8,128)S(1)}, f32[392,128]{1,0:T(8,128)S(1)}, u32[]{:S(2)}, u32[]{:S(2)}) collective-permute-start(f32[392,128]{1,0:T(8,128)S(1)} %get-tuple-element.68), channel_id=1, source_target_pairs={{0,224},{32,64},{64,32},{96,128},{128,96},{160,192},{192,160},{224... | collective-permute-start | bytes 602120 | tf_op jit(solution)/shard_map/ppermute | solution.py:558
  51.7 13.8 %collective-permute-start.15 = (f32[280,128]{1,0:T(8,128)S(1)}, f32[280,128]{1,0:T(8,128)S(1)}, u32[]{:S(2)}, u32[]{:S(2)}) collective-permute-start(f32[280,128]{1,0:T(8,128)S(1)} %get-tuple-element.70), channel_id=1, source_target_pairs={{0,224},{32,64},{64,32},{96,128},{128,96},{160,192},{192,160},{224... | collective-permute-start | bytes 430088 | tf_op jit(solution)/shard_map/ppermute | solution.py:558
  60.8 5.3 %collective-permute-start.16 = (f32[184,128]{1,0:T(8,128)S(1)}, f32[184,128]{1,0:T(8,128)S(1)}, u32[]{:S(2)}, u32[]{:S(2)}) collective-permute-start(f32[184,128]{1,0:T(8,128)S(1)} %get-tuple-element.76), channel_id=1, source_target_pairs={{0,32},{32,0},{64,96},{96,64},{128,160},{160,128},{192,224},{224,1... | collective-permute-start | bytes 282632 | tf_op jit(solution)/shard_map/ppermute | solution.py:553
  62.5 4.0 %collective-permute-start.17 = (f32[184,128]{1,0:T(8,128)S(1)}, f32[184,128]{1,0:T(8,128)S(1)}, u32[]{:S(2)}, u32[]{:S(2)}) collective-permute-start(f32[184,128]{1,0:T(8,128)S(1)} %get-tuple-element.77), channel_id=1, source_target_pairs={{0,224},{32,64},{64,32},{96,128},{128,96},{160,192},{192,160},{224... | collective-permute-start | bytes 282632 | tf_op jit(solution)/shard_map/ppermute | solution.py:558

commit v3 on v2

--- a/solution.py
+++ b/solution.py
@@ -37,7 +37,7 @@
 BAND_LATE = -(-H * (H + 1) // 8) * 8
 REACHES = [(j, H + 1 - j, (j - 1) * (2 * H + 2) - (j - 1) * j) for j in range(1, H + 1)]
 LANE_COARSE = C * H
-PIECES = 4
+PIECES = 16
 FIT = 16 * 2**20
 
 f32 = jnp.float32
@@ -236,11 +236,14 @@
         dst[H * (H + 1) :, :] = jnp.zeros((BAND_LATE - H * (H + 1), L), f32)
 
 
-def place_late(ext, above, below):
+def place_late(ext, a, wext, above, below):
     for j, reach, at in REACHES:
         for msg, row in ((above, CR0 - j), (below, CR0 + C + j - 1)):
-            ext[row, CC0 - reach : CC0, :] = msg[at : at + reach, :]
-            ext[row, CC0 + C : CC0 + C + reach, :] = msg[at + reach : at + 2 * reach, :]
+            for lo, first in ((at, CC0 - reach), (at + reach, CC0 + C)):
+                cols = slice(first, first + reach)
+                values = msg[lo : lo + reach, :]
+                ext[row, cols, :] = values
+                a[row, cols, :] = wext[row, cols, :] * values
 
 
 def weight(mass):
@@ -316,7 +319,7 @@
     token[...] = jnp.zeros((8, L), f32)
 
 
-def before(u_in, f_in, w_in, v1_in, v2_in, v3_in, cl_in, a4, re, ro, be, bo, ce, co, u, f, w, v1, v2, v3, cl, l_even, l_odd, rim_even, rim_odd, wl, wr, wc, line):
+def from_lanes(u_in, f_in, w_in, v1_in, v2_in, v3_in, cl_in, a4, re, ro, u, f, w, v1, v2, v3, cl, wl, wr):
     del u_in, f_in, w_in, v1_in, v2_in, v3_in, cl_in
 
     def lanes(left, right):
@@ -335,8 +338,25 @@
 
             lax.fori_loop(0, N // 8, group, 0)
 
+    either(parity("lane"), lambda: lanes(ro, re), lambda: lanes(re, ro))
+    for src, dst, k in ((u, v1, 1), (v1, v2, 2), (v2, v3, 3)):
+        sweep_rows(src, dst, w, f, R0 + k, R1 - k, EDGES)
+
+    def rims(i, carry):
+        row = R0 + RATIO * i
+        left = defect_sum(v3, f, a4, row, C0 - 4, C0 + 4)
+        right = defect_sum(v3, f, a4, row, C1 - 4, C1 + 4)
+        cl[i, 0:1, :] = jnp.sum(left[4:8, :], axis=0, keepdims=True) * (1.0 / RATIO)
+        cl[i, C - 1 : C, :] = jnp.sum(right[0:4, :], axis=0, keepdims=True) * (1.0 / RATIO)
+        return carry
+
+    lax.fori_loop(1, C - 1, rims, 0)
+
+
+def before(u_in, f_in, w_in, v1_in, v2_in, v3_in, cl_in, a4, be, bo, ce, co, u, f, w, v1, v2, v3, cl, l_even, l_odd, rim_even, rim_odd, wc, line):
+    del u_in, f_in, w_in, v1_in, v2_in, v3_in, cl_in
+
     lane_even, band_even = parity("lane"), parity("band")
-    either(lane_even, lambda: lanes(ro, re), lambda: lanes(re, ro))
 
     def bands(above, below, above_c, below_c):
         own = slice(C0, C1)
@@ -365,20 +385,9 @@
         reach = BEFORE + 1 - k
         sweep_rows(src, dst, w, f, R0 - reach, R0 + k, FULL)
         sweep_rows(src, dst, w, f, R1 - k, R1 + reach, FULL)
-        sweep_rows(src, dst, w, f, R0 + k, R1 - k, EDGES)
 
     for i in (0, C - 1):
         cl[i] = gather_columns(line, defect_sum(v3, f, a4, R0 + RATIO * i, C0, C1))
-
-    def rims(i, carry):
-        row = R0 + RATIO * i
-        left = defect_sum(v3, f, a4, row, C0 - 4, C0 + 4)
-        right = defect_sum(v3, f, a4, row, C1 - 4, C1 + 4)
-        cl[i, 0:1, :] = jnp.sum(left[4:8, :], axis=0, keepdims=True) * (1.0 / RATIO)
-        cl[i, C - 1 : C, :] = jnp.sum(right[0:4, :], axis=0, keepdims=True) * (1.0 / RATIO)
-        return carry
-
-    lax.fori_loop(1, C - 1, rims, 0)
 
     def out_lanes(right, left):
         pack_coarse_lanes(cl, right, left, 0)
@@ -455,7 +464,7 @@
     )
 
 
-def between(v_in, lext_in, mext, mbe, mbo, le, lo, rbe, rbo, v, lext, wext, ext):
+def between(v_in, lext_in, mext, mbe, mbo, le, lo, rbe, rbo, v, lext, wext, a, ext):
     del v_in, lext_in
 
     def lanes(left, right):
@@ -492,29 +501,30 @@
     either(parity("band"), lambda: bands(mbo, mbe), lambda: bands(mbe, mbo))
 
     def weights(r):
-        wext[r] = weight(ext[r])
+        wc = weight(ext[r])
+        wext[r] = wc
+        a[r] = wc * lext[r]
 
     loop(CR, 2, weights)
 
 
-def after(v, f, w, wext, lext_in, lbe, lbo, result, lext, a, b, wide, t, s, out, sems):
-    del lext_in
+def after(v, f, w, wext, lext_in, a_in, lbe, lbo, result, lext, a, b, wide, t, s, out, sems):
+    del lext_in, a_in
     either(
         parity("band"),
-        lambda: place_late(lext, lbo, lbe),
-        lambda: place_late(lext, lbe, lbo),
+        lambda: place_late(lext, a, wext, lbo, lbe),
+        lambda: place_late(lext, a, wext, lbe, lbo),
     )
 
-    def first(r):
-        a[r] = wext[r] * lext[r]
-
-    loop(CR, 2, first)
     src, dst = a, b
     for k in range(1, INNER):
-        segments = ((8, 24), (24, 48)) if k <= 8 else ((16, 40),)
+        first = CC0 - H + k
+        wide_by = -(-(CR - 2 * k) // 8) * 8
+        segments = ((first, first + 16), (first + 16, first + wide_by)) if wide_by > 24 else ((first, first + 24),)
         sweep_rows(src, dst, wext, lext, k, CR - k, segments)
         src, dst = dst, src
-    for i in range(-1, C + 1):
+
+    def correct(i):
         row = src[CR0 + i, CC0 - 1 : CC0 + C + 1, :]
         for k in range(RATIO):
             wide[pl.ds(k, C + 2, stride=RATIO), :] = row
@@ -522,7 +532,6 @@
             q = i * RATIO + k
             if -AFTER <= q < N + AFTER:
                 t[R0 + q, C0 - 4 : C1 + 4, :] = v[R0 + q, C0 - 4 : C1 + 4, :] + wide[...]
-    sweep_rows(t, s, w, f, R0 - 1, R1 + 1, FULL, per=2)
 
     def last(r, carry):
         for lo, hi in ((0, 32), (32, 64)):
@@ -538,9 +547,17 @@
         return carry
 
     copies = []
+    rows = N // PIECES
+    corrected, swept = -1, R0 - 1
     for piece in range(PIECES):
-        rows = N // PIECES
-        lax.fori_loop(piece * rows // 4, (piece + 1) * rows // 4, last, 0)
+        end = (piece + 1) * rows
+        upto = min(C, (end + 1) // RATIO)
+        for i in range(corrected, upto + 1):
+            correct(i)
+        corrected = upto + 1
+        sweep_rows(t, s, w, f, swept, R0 + end + 1, FULL)
+        swept = R0 + end + 1
+        lax.fori_loop(piece * rows // 4, end // 4, last, 0)
         span = pl.ds(piece * rows, rows)
         copies.append(pltpu.make_async_copy(out.at[span], result.at[span], sems.at[piece]))
         copies[-1].start()
@@ -606,31 +623,45 @@
     )(cm, redges, rnear, racross)
     rmbo, rmbe = swap_odd(mbo, "band"), swap_even(mbe, "band")
 
+    u, f, w, v1, v2, v3, cl = call(
+        from_lanes,
+        [fine] * 6 + [own_coarse],
+        [VM] * 10,
+        [pltpu.VMEM((N * DF, L), f32), pltpu.VMEM((N * DF, L), f32)],
+        aliases={k: k for k in range(7)},
+        flops=10**7,
+    )(u, f, w, v1, v2, v3, cl, a4, re, ro)
+
     u, f, w, v1, v2, v3, cl, le, lo, rime, rimo = call(
         before,
         [fine] * 6 + [own_coarse, lane_coarse, lane_coarse, early, early],
-        [VM] * 14,
-        [pltpu.VMEM((N * DF, L), f32), pltpu.VMEM((N * DF, L), f32), pltpu.VMEM(corner.shape, f32), line],
+        [VM] * 12,
+        [pltpu.VMEM(corner.shape, f32), line],
         aliases={k: k for k in range(7)},
         flops=10**8,
-    )(u, f, w, v1, v2, v3, cl, a4, re, ro, rbe, rbo, rce, rco)
+    )(u, f, w, v1, v2, v3, cl, a4, rbe, rbo, rce, rco)
     rlo, rle = swap_odd(lo, "lane"), swap_even(le, "lane")
     rrimo, rrime = swap_odd(rimo, "band"), swap_even(rime, "band")
     lext, lbe, lbo = call(coarse_bands, [coarse, band_late, band_late], [VM] * 3)(cl, rle, rlo)
     rlbo, rlbe = swap_odd(lbo, "band"), swap_even(lbe, "band")
-    v3, lext, wext = call(
-        between, [fine, coarse, coarse], [VM] * 9, [coarse_buf], aliases={0: 0, 1: 1}, flops=10**7
+    v3, lext, wext, first = call(
+        between,
+        [fine, coarse, coarse, coarse],
+        [VM] * 9,
+        [coarse_buf],
+        aliases={0: 0, 1: 1},
+        flops=10**7,
     )(v3, lext, mext, rmbe, rmbo, rle, rlo, rrime, rrimo)
 
-    out, _ = call(
+    out, *_ = call(
         after,
-        [own, coarse],
-        [VM] * 7,
-        [coarse_buf] * 2 + [pltpu.VMEM((N + 8, L), f32), fine_buf, fine_buf, own_buf, dma((PIECES,))],
+        [own, coarse, coarse],
+        [VM] * 8,
+        [coarse_buf] + [pltpu.VMEM((N + 8, L), f32), fine_buf, fine_buf, own_buf, dma((PIECES,))],
         flops=10**8,
-        aliases={4: 1},
+        aliases={4: 1, 5: 2},
         result=True,
-    )(v3, f, w, wext, lext, rlbe, rlbo)
+    )(v3, f, w, wext, lext, first, rlbe, rlbo)
     return out
 
 

time: 71.9 us -> 72.4 us (level)
  starting transfers between devices: 36.8 us -> 37.8 us
    ppermute x7, starting transfers between devices: 19.1 us -> 22.2 us  [swap_odd(): lax.ppermute(x, axis, [(i, (i + 1) % n if i % 2 else (i - 1) % n) for i i...]
    ppermute x9, starting transfers between devices: 16.3 us -> 14.2 us  [swap_even(): return lax.ppermute(x, axis, [(i, i ^ 1) for i in range(n)])]
    pallas_call x1, Pallas kernels: 2 us -> 0.62 us  [shards(): call(before, [fine] * 6 + [own_coarse, lane_coarse, lane_coarse, early, e...]
    pallas_call x2 -> x3, Pallas kernels: 5.87 us -> 6.56 us  [the longest x1 4.68 us: shards(): call(after, [own, coarse, coarse], [VM] * 8, [coarse_buf] + [pltpu.VMEM((...]
where the time goes in v3:
time: 72.4 us; the launch traced here: 72.2 us
  starting transfers between devices  37.8 us (52%)
  waiting for transfers between devices  18.4 us (25%)
  Pallas kernels  16 us (22%)
    ppermute x7, starting transfers between devices, swap_odd(): lax.ppermute(x, axis, [(i, (i + 1) % n if i % 2 else (i - 1) % n) for i i...  22.2 us
    ppermute x9, starting transfers between devices, swap_even(): return lax.ppermute(x, axis, [(i, i ^ 1) for i in range(n)])  14.2 us
    ppermute x7, waiting for transfers between devices, swap_odd(): lax.ppermute(x, axis, [(i, (i + 1) % n if i % 2 else (i - 1) % n) for i i...  12.1 us
    ppermute x9, waiting for transfers between devices, swap_even(): return lax.ppermute(x, axis, [(i, i ^ 1) for i in range(n)])  6.2 us
    pallas_call x1, Pallas kernels, shards(): call(prepare, [fine] * 7 + [own_coarse, sds(8, L)], [HBM, HBM, VM], [own_...  6.13 us
    pallas_call x1, Pallas kernels, shards(): call(after, [own, coarse, coarse], [VM] * 8, [coarse_buf] + [pltpu.VMEM((...  4.68 us
    pallas_call x1, Pallas kernels, shards(): call(pack_fine, [lane_msg, lane_msg, band_msg, band_msg, own, own_coarse,...  2.47 us
  transfers between devices with their start and end apart: 18, of which 4 were waited for; matrix products, arithmetic and copies ran while one was open for 0% of the time, Pallas kernels for 12%

profile of v3, /device:TPU:1, one launch (start us, length us, event | category | flops | bytes accessed | tf_op | source)
XLA Modules:
  0.0 72.2 jit_solution(14897292584181276002)
XLA Ops:
  0.0 2.5 %shard_map.37 = (f32[640,128]{1,0:T(8,128)S(1)}, f32[640,128]{1,0:T(8,128)S(1)}, f32[10,64,128]{2,1,0:T(8,128)S(1)}, f32[10,64,128]{2,1,0:T(8,128)S(1)}, f32[64,...) custom-call(f32[64,64,128]{2,1,0:T(8,128)} %load.3, ...), custom_call_target="tpu_custom_call" | custom-call | flops 1000000 | bytes 8000000 | tf_op jit(solution)/shard_map/pallas_call | solution.py:591
  2.5 2.1 %collective-permute-start = (f32[640,128]{1,0:T(8,128)S(1)}, f32[640,128]{1,0:T(8,128)S(1)}, u32[]{:S(2)}, u32[]{:S(2)}) collective-permute-start(f32[640,128]{1,0:T(8,128)S(1)} %get-tuple-element.59), channel_id=1, source_target_pairs={{0,1},{1,0},{2,3},{3,2},{4,5},{5,4},{6,7},{7,6},{8,9},{9,8},{10,11... | collective-permute-start | bytes 983048 | tf_op jit(solution)/shard_map/ppermute | solution.py:570
  4.6 10.9 %collective-permute-start.1 = (f32[640,128]{1,0:T(8,128)S(1)}, f32[640,128]{1,0:T(8,128)S(1)}, u32[]{:S(2)}, u32[]{:S(2)}) collective-permute-start(f32[640,128]{1,0:T(8,128)S(1)} %get-tuple-element.60), channel_id=1, source_target_pairs={{0,31},{1,2},{2,1},{3,4},{4,3},{5,6},{6,5},{7,8},{8,7},{9,10},{10,... | collective-permute-start | bytes 983048 | tf_op jit(solution)/shard_map/ppermute | solution.py:575
  15.5 1.2 %collective-permute-start.2 = (f32[10,64,128]{2,1,0:T(8,128)S(1)}, f32[10,64,128]{2,1,0:T(8,128)S(1)}, u32[]{:S(2)}, u32[]{:S(2)}) collective-permute-start(f32[10,64,128]{2,1,0:T(8,128)S(1)} %get-tuple-element.68), channel_id=1, source_target_pairs={{0,32},{32,0},{64,96},{96,64},{128,160},{160,128},{192,224},{224,1... | collective-permute-start | bytes 983048 | tf_op jit(solution)/shard_map/ppermute | solution.py:570
  16.7 0.0 collective-permute-start.8
  16.7 0.6 collective-permute-start.3
  17.4 6.2 %collective-permute-done.8.edges = f32[416,128]{1,0:T(8,128)S(1)} collective-permute-done((f32[416,128]{1,0:T(8,128)S(1)}, f32[416,128]{1,0:T(8,128)S(1)}, u32[]{:S(2)}, u32[]{:S(2)}) %collective-permute-start.8) | collective-permute-done | bytes 213024 | tf_op jit(solution)/shard_map/ppermute | solution.py:570
  23.5 0.7 collective-permute-start.10
  24.2 6.1 %shard_map.38 = (f32[72,88,128]{2,1,0:T(8,128)S(1)}, f32[72,88,128]{2,1,0:T(8,128)S(1)}, f32[72,88,128]{2,1,0:T(8,128)S(1)}, f32[72,88,128]{2,1,0:T(8,128)S(1)},...) custom-call(f32[64,64,128]{2,1,0:T(8,128)} %load.3, ...), custom_call_target="tpu_custom_call" | custom-call | flops 100000000 | bytes 8000000 | tf_op jit(solution)/shard_map/pallas_call | solution.py:610
  30.4 0.0 collective-permute-done.re.m_even
  30.4 0.0 collective-permute-done.1.ro.m_odd
  30.4 1.4 %collective-permute-start.4 = (f32[60,128]{1,0:T(8,128)S(1)}, f32[60,128]{1,0:T(8,128)S(1)}, u32[]{:S(2)}, u32[]{:S(2)}) collective-permute-start(f32[60,128]{1,0:T(8,128)S(1)} %get-tuple-element.71), channel_id=1, source_target_pairs={{0,32},{32,0},{64,96},{96,64},{128,160},{160,128},{192,224},{224,1... | collective-permute-start | bytes 92168 | tf_op jit(solution)/shard_map/ppermute | solution.py:570
  31.8 1.8 %collective-permute-start.5 = (f32[60,128]{1,0:T(8,128)S(1)}, f32[60,128]{1,0:T(8,128)S(1)}, u32[]{:S(2)}, u32[]{:S(2)}) collective-permute-start(f32[60,128]{1,0:T(8,128)S(1)} %get-tuple-element.72), channel_id=1, source_target_pairs={{0,224},{32,64},{64,32},{96,128},{128,96},{160,192},{192,160},{224... | collective-permute-start | bytes 92168 | tf_op jit(solution)/shard_map/ppermute | solution.py:575
  33.6 0.0 collective-permute-done.10
  33.6 0.7 collective-permute-start.9
  34.3 0.0 collective-permute-done.2.be
  34.3 6.5 %collective-permute-start.11 = (f32[208,128]{1,0:T(8,128)S(1)}, f32[208,128]{1,0:T(8,128)S(1)}, u32[]{:S(2)}, u32[]{:S(2)}) collective-permute-start(f32[208,128]{1,0:T(8,128)S(1)} %collective-permute-done.10), channel_id=1, source_target_pairs={{0,1},{1,0},{2,3},{3,2},{4,5},{5,4},{6,7},{7,6},{8,9},{9,8},{10,11... | collective-permute-start | bytes 319496 | tf_op jit(solution)/shard_map/ppermute | solution.py:570
  40.8 1.3 %shard_map.39 = (f32[72,88,128]{2,1,0:T(8,128)S(1)}, f32[72,88,128]{2,1,0:T(8,128)S(1)}, f32[72,88,128]{2,1,0:T(8,128)S(1)}, f32[72,88,128]{2,1,0:T(8,128)S(1)},...) custom-call(f32[72,88,128]{2,1,0:T(8,128)S(1)} %get-tuple-element.51, ...), custom_call_target="tpu_custom_call", output_to_operand_aliasing={{0}: (0, {}), {1}: (1, {}), {2}: (2, {}), {3}: (3, {}), {4}... | custom-call | flops 10000000 | bytes 8000000 | tf_op jit(solution)/shard_map/pallas_call | solution.py:626
  42.1 0.0 collective-permute-done.3.bo
  42.1 0.0 collective-permute-done.4.ce
  42.1 0.0 collective-permute-done.5.co
  42.2 0.6 shard_map.41
  42.8 0.1 collective-permute-start.6
  42.9 1.7 %collective-permute-start.14 = (f32[280,128]{1,0:T(8,128)S(1)}, f32[280,128]{1,0:T(8,128)S(1)}, u32[]{:S(2)}, u32[]{:S(2)}) collective-permute-start(f32[280,128]{1,0:T(8,128)S(1)} %get-tuple-element.84), channel_id=1, source_target_pairs={{0,32},{32,0},{64,96},{96,64},{128,160},{160,128},{192,224},{224,1... | collective-permute-start | bytes 430088 | tf_op jit(solution)/shard_map/ppermute | solution.py:570
  44.6 5.1 %collective-permute-start.7 = (f32[272,128]{1,0:T(8,128)S(1)}, f32[272,128]{1,0:T(8,128)S(1)}, u32[]{:S(2)}, u32[]{:S(2)}) collective-permute-start(f32[272,128]{1,0:T(8,128)S(1)} %get-tuple-element.76), channel_id=1, source_target_pairs={{0,31},{1,2},{2,1},{3,4},{4,3},{5,6},{6,5},{7,8},{8,7},{9,10},{10,... | collective-permute-start | bytes 417800 | tf_op jit(solution)/shard_map/ppermute | solution.py:575
  49.6 0.0 collective-permute-done.9.near
  49.6 0.0 collective-permute-done.11.across
  49.6 0.1 shard_map.44
  49.7 0.5 collective-permute-start.12
  50.2 1.5 %collective-permute-start.13 = (f32[392,128]{1,0:T(8,128)S(1)}, f32[392,128]{1,0:T(8,128)S(1)}, u32[]{:S(2)}, u32[]{:S(2)}) collective-permute-start(f32[392,128]{1,0:T(8,128)S(1)} %get-tuple-element.83), channel_id=1, source_target_pairs={{0,224},{32,64},{64,32},{96,128},{128,96},{160,192},{192,160},{224... | collective-permute-start | bytes 602120 | tf_op jit(solution)/shard_map/ppermute | solution.py:575
  51.6 0.0 collective-permute-done.6.re.le
  51.6 0.3 collective-permute-start.15
  51.9 9.4 %collective-permute-done.7.ro.lo = f32[272,128]{1,0:T(8,128)S(1)} collective-permute-done((f32[272,128]{1,0:T(8,128)S(1)}, f32[272,128]{1,0:T(8,128)S(1)}, u32[]{:S(2)}, u32[]{:S(2)}) %collective-permute-start.7) | collective-permute-done | bytes 139296 | tf_op jit(solution)/shard_map/ppermute | solution.py:575
  61.3 0.1 shard_map.42
  61.4 0.7 collective-permute-start.16
  62.1 0.0 collective-permute-done.14.rbe
  62.1 2.1 %collective-permute-start.17 = (f32[184,128]{1,0:T(8,128)S(1)}, f32[184,128]{1,0:T(8,128)S(1)}, u32[]{:S(2)}, u32[]{:S(2)}) collective-permute-start(f32[184,128]{1,0:T(8,128)S(1)} %get-tuple-element.93), channel_id=1, source_target_pairs={{0,224},{32,64},{64,32},{96,128},{128,96},{160,192},{192,160},{224... | collective-permute-start | bytes 282632 | tf_op jit(solution)/shard_map/ppermute | solution.py:575
  64.2 1.2 %collective-permute-done.15.rbo = f32[280,128]{1,0:T(8,128)S(1)} collective-permute-done((f32[280,128]{1,0:T(8,128)S(1)}, f32[280,128]{1,0:T(8,128)S(1)}, u32[]{:S(2)}, u32[]{:S(2)}) %collective-permute-start.15) | collective-permute-done | bytes 143392 | tf_op jit(solution)/shard_map/ppermute | solution.py:575
  65.4 0.0 collective-permute-done.12.mbe
  65.4 0.0 collective-permute-done.13.mbo
  65.4 0.6 shard_map.45
  66.0 0.0 collective-permute-done.16.lbe
  66.0 1.5 %collective-permute-done.17.lbo = f32[184,128]{1,0:T(8,128)S(1)} collective-permute-done((f32[184,128]{1,0:T(8,128)S(1)}, f32[184,128]{1,0:T(8,128)S(1)}, u32[]{:S(2)}, u32[]{:S(2)}) %collective-permute-start.17) | collective-permute-done | bytes 94240 | tf_op jit(solution)/shard_map/ppermute | solution.py:575
  67.6 4.7 %shard_map.46 = (f32[64,64,128]{2,1,0:T(8,128)}, f32[42,56,128]{2,1,0:T(8,128)S(1)}, f32[42,56,128]{2,1,0:T(8,128)S(1)}) custom-call(f32[72,88,128]{2,1,0:T(8,128)S(1)} %get-tuple-element.86.v, f32[72,88,128]{2,1,0:T(8,128)S(1)} %get-tuple-element.87.f, f32[72,88,128]{2,1,0:T(8,128)S(1)} %get-tuple-element.88.w, ...), custom_call_target="tpu_custom_call", output_to_operand_aliasing={{1}: (4, {}), {2}: (5, {})} | custom-call | flops 100000000 | bytes 8000000 | tf_op jit(solution)/shard_map/pallas_call | solution.py:656
  (2 shorter events, 0.0 us)
Async XLA Ops:
  2.5 27.9 %collective-permute-start = (f32[640,128]{1,0:T(8,128)S(1)}, f32[640,128]{1,0:T(8,128)S(1)}, u32[]{:S(2)}, u32[]{:S(2)}) collective-permute-start(f32[640,128]{1,0:T(8,128)S(1)} %get-tuple-element.59), channel_id=1, source_target_pairs={{0,1},{1,0},{2,3},{3,2},{4,5},{5,4},{6,7},{7,6},{8,9},{9,8},{10,11... | collective-permute-start | bytes 983048 | tf_op jit(solution)/shard_map/ppermute | solution.py:570
  4.6 25.8 %collective-permute-start.1 = (f32[640,128]{1,0:T(8,128)S(1)}, f32[640,128]{1,0:T(8,128)S(1)}, u32[]{:S(2)}, u32[]{:S(2)}) collective-permute-start(f32[640,128]{1,0:T(8,128)S(1)} %get-tuple-element.60), channel_id=1, source_target_pairs={{0,31},{1,2},{2,1},{3,4},{4,3},{5,6},{6,5},{7,8},{8,7},{9,10},{10,... | collective-permute-start | bytes 983048 | tf_op jit(solution)/shard_map/ppermute | solution.py:575
  15.5 18.8 %collective-permute-start.2 = (f32[10,64,128]{2,1,0:T(8,128)S(1)}, f32[10,64,128]{2,1,0:T(8,128)S(1)}, u32[]{:S(2)}, u32[]{:S(2)}) collective-permute-start(f32[10,64,128]{2,1,0:T(8,128)S(1)} %get-tuple-element.68), channel_id=1, source_target_pairs={{0,32},{32,0},{64,96},{96,64},{128,160},{160,128},{192,224},{224,1... | collective-permute-start | bytes 983048 | tf_op jit(solution)/shard_map/ppermute | solution.py:570
  16.7 6.8 %collective-permute-start.8 = (f32[416,128]{1,0:T(8,128)S(1)}, f32[416,128]{1,0:T(8,128)S(1)}, u32[]{:S(2)}, u32[]{:S(2)}) collective-permute-start(f32[416,128]{1,0:T(8,128)S(1)} %get-tuple-element.79), channel_id=1, source_target_pairs={{0,1},{1,0},{2,3},{3,2},{4,5},{5,4},{6,7},{7,6},{8,9},{9,8},{10,11... | collective-permute-start | bytes 638984 | tf_op jit(solution)/shard_map/ppermute | solution.py:570
  16.7 25.4 %collective-permute-start.3 = (f32[10,64,128]{2,1,0:T(8,128)S(1)}, f32[10,64,128]{2,1,0:T(8,128)S(1)}, u32[]{:S(2)}, u32[]{:S(2)}) collective-permute-start(f32[10,64,128]{2,1,0:T(8,128)S(1)} %get-tuple-element.69), channel_id=1, source_target_pairs={{0,224},{32,64},{64,32},{96,128},{128,96},{160,192},{192,160},{224... | collective-permute-start | bytes 983048 | tf_op jit(solution)/shard_map/ppermute | solution.py:575
  23.5 10.1 %collective-permute-start.10 = (f32[208,128]{1,0:T(8,128)S(1)}, f32[208,128]{1,0:T(8,128)S(1)}, u32[]{:S(2)}, u32[]{:S(2)}) collective-permute-start(f32[208,128]{1,0:T(8,128)S(1)} %shard_map.43), channel_id=1, source_target_pairs={{14,17},{30,1},{17,14},{1,30},{46,49},{62,33},{49,46},{33,62},{78,... | collective-permute-start | bytes 319496 | tf_op jit(solution)/shard_map/ppermute | solution.py:607
  30.4 11.7 %collective-permute-start.4 = (f32[60,128]{1,0:T(8,128)S(1)}, f32[60,128]{1,0:T(8,128)S(1)}, u32[]{:S(2)}, u32[]{:S(2)}) collective-permute-start(f32[60,128]{1,0:T(8,128)S(1)} %get-tuple-element.71), channel_id=1, source_target_pairs={{0,32},{32,0},{64,96},{96,64},{128,160},{160,128},{192,224},{224,1... | collective-permute-start | bytes 92168 | tf_op jit(solution)/shard_map/ppermute | solution.py:570
  31.8 10.3 %collective-permute-start.5 = (f32[60,128]{1,0:T(8,128)S(1)}, f32[60,128]{1,0:T(8,128)S(1)}, u32[]{:S(2)}, u32[]{:S(2)}) collective-permute-start(f32[60,128]{1,0:T(8,128)S(1)} %get-tuple-element.72), channel_id=1, source_target_pairs={{0,224},{32,64},{64,32},{96,128},{128,96},{160,192},{192,160},{224... | collective-permute-start | bytes 92168 | tf_op jit(solution)/shard_map/ppermute | solution.py:575
  33.6 16.0 %collective-permute-start.9 = (f32[208,128]{1,0:T(8,128)S(1)}, f32[208,128]{1,0:T(8,128)S(1)}, u32[]{:S(2)}, u32[]{:S(2)}) collective-permute-start(f32[208,128]{1,0:T(8,128)S(1)} %get-tuple-element.80), channel_id=1, source_target_pairs={{1,2},{3,4},{5,6},{7,8},{9,10},{11,12},{13,14},{17,18},{19,20},{21... | collective-permute-start | bytes 319496 | tf_op jit(solution)/shard_map/ppermute | solution.py:604
  34.3 15.3 %collective-permute-start.11 = (f32[208,128]{1,0:T(8,128)S(1)}, f32[208,128]{1,0:T(8,128)S(1)}, u32[]{:S(2)}, u32[]{:S(2)}) collective-permute-start(f32[208,128]{1,0:T(8,128)S(1)} %collective-permute-done.10), channel_id=1, source_target_pairs={{0,1},{1,0},{2,3},{3,2},{4,5},{5,4},{6,7},{7,6},{8,9},{9,8},{10,11... | collective-permute-start | bytes 319496 | tf_op jit(solution)/shard_map/ppermute | solution.py:570
  42.8 8.9 %collective-permute-start.6 = (f32[272,128]{1,0:T(8,128)S(1)}, f32[272,128]{1,0:T(8,128)S(1)}, u32[]{:S(2)}, u32[]{:S(2)}) collective-permute-start(f32[272,128]{1,0:T(8,128)S(1)} %get-tuple-element.75), channel_id=1, source_target_pairs={{0,1},{1,0},{2,3},{3,2},{4,5},{5,4},{6,7},{7,6},{8,9},{9,8},{10,11... | collective-permute-start | bytes 417800 | tf_op jit(solution)/shard_map/ppermute | solution.py:570
  42.9 19.2 %collective-permute-start.14 = (f32[280,128]{1,0:T(8,128)S(1)}, f32[280,128]{1,0:T(8,128)S(1)}, u32[]{:S(2)}, u32[]{:S(2)}) collective-permute-start(f32[280,128]{1,0:T(8,128)S(1)} %get-tuple-element.84), channel_id=1, source_target_pairs={{0,32},{32,0},{64,96},{96,64},{128,160},{160,128},{192,224},{224,1... | collective-permute-start | bytes 430088 | tf_op jit(solution)/shard_map/ppermute | solution.py:570
  44.6 16.7 %collective-permute-start.7 = (f32[272,128]{1,0:T(8,128)S(1)}, f32[272,128]{1,0:T(8,128)S(1)}, u32[]{:S(2)}, u32[]{:S(2)}) collective-permute-start(f32[272,128]{1,0:T(8,128)S(1)} %get-tuple-element.76), channel_id=1, source_target_pairs={{0,31},{1,2},{2,1},{3,4},{4,3},{5,6},{6,5},{7,8},{8,7},{9,10},{10,... | collective-permute-start | bytes 417800 | tf_op jit(solution)/shard_map/ppermute | solution.py:575
  49.7 15.7 %collective-permute-start.12 = (f32[392,128]{1,0:T(8,128)S(1)}, f32[392,128]{1,0:T(8,128)S(1)}, u32[]{:S(2)}, u32[]{:S(2)}) collective-permute-start(f32[392,128]{1,0:T(8,128)S(1)} %get-tuple-element.82), channel_id=1, source_target_pairs={{0,32},{32,0},{64,96},{96,64},{128,160},{160,128},{192,224},{224,1... | collective-permute-start | bytes 602120 | tf_op jit(solution)/shard_map/ppermute | solution.py:570
  50.2 15.3 %collective-permute-start.13 = (f32[392,128]{1,0:T(8,128)S(1)}, f32[392,128]{1,0:T(8,128)S(1)}, u32[]{:S(2)}, u32[]{:S(2)}) collective-permute-start(f32[392,128]{1,0:T(8,128)S(1)} %get-tuple-element.83), channel_id=1, source_target_pairs={{0,224},{32,64},{64,32},{96,128},{128,96},{160,192},{192,160},{224... | collective-permute-start | bytes 602120 | tf_op jit(solution)/shard_map/ppermute | solution.py:575
  51.6 13.8 %collective-permute-start.15 = (f32[280,128]{1,0:T(8,128)S(1)}, f32[280,128]{1,0:T(8,128)S(1)}, u32[]{:S(2)}, u32[]{:S(2)}) collective-permute-start(f32[280,128]{1,0:T(8,128)S(1)} %get-tuple-element.85), channel_id=1, source_target_pairs={{0,224},{32,64},{64,32},{96,128},{128,96},{160,192},{192,160},{224... | collective-permute-start | bytes 430088 | tf_op jit(solution)/shard_map/ppermute | solution.py:575
  61.4 4.7 %collective-permute-start.16 = (f32[184,128]{1,0:T(8,128)S(1)}, f32[184,128]{1,0:T(8,128)S(1)}, u32[]{:S(2)}, u32[]{:S(2)}) collective-permute-start(f32[184,128]{1,0:T(8,128)S(1)} %get-tuple-element.92), channel_id=1, source_target_pairs={{0,32},{32,0},{64,96},{96,64},{128,160},{160,128},{192,224},{224,1... | collective-permute-start | bytes 282632 | tf_op jit(solution)/shard_map/ppermute | solution.py:570
  62.1 5.5 %collective-permute-start.17 = (f32[184,128]{1,0:T(8,128)S(1)}, f32[184,128]{1,0:T(8,128)S(1)}, u32[]{:S(2)}, u32[]{:S(2)}) collective-permute-start(f32[184,128]{1,0:T(8,128)S(1)} %get-tuple-element.93), channel_id=1, source_target_pairs={{0,224},{32,64},{64,32},{96,128},{128,96},{160,192},{192,160},{224... | collective-permute-start | bytes 282632 | tf_op jit(solution)/shard_map/ppermute | solution.py:575

commit v4 on v3

--- a/solution.py
+++ b/solution.py
@@ -285,28 +285,15 @@
     return total
 
 
-def prepare(load, start, mass, u, f, w, a4, v1, v2, v3, cl, token, load_in, start_in, line, sems):
-    copies = [
-        pltpu.make_async_copy(load, load_in, sems.at[0]),
-        pltpu.make_async_copy(start, start_in, sems.at[1]),
-    ]
-    for c in copies:
-        c.start()
-
-    def weights(r):
+def prepare(load, start, mass, u, f, w, a4, v1, v2, v3, cl, token, line):
+    def own(r):
         a = 4.0 + mass[r]
         a4[R0 + r, C0:C1, :] = a
         w[R0 + r, C0:C1, :] = 0.8 / a
-
-    loop(N, 2, weights)
-    for c in copies:
-        c.wait()
-
-    def place(r):
-        f[R0 + r, C0:C1, :] = load_in[r]
-        u[R0 + r, C0:C1, :] = start_in[r]
-
-    loop(N, 2, place)
+        f[R0 + r, C0:C1, :] = load[r]
+        u[R0 + r, C0:C1, :] = start[r]
+
+    loop(N, 2, own)
     sweep_rows(u, v1, w, f, R0 + 1, R1 - 1, FULL)
     sweep_rows(v1, v2, w, f, R0 + 2, R1 - 2, FULL)
     sweep_rows(v2, v3, w, f, R0 + 3, R1 - 3, FULL)
@@ -576,6 +563,7 @@
 
 
 def shards(load, start, mass):
+    raw = (load, start)
     load, start, mass = (pltpu.with_memory_space_constraint(x, pltpu.HBM) for x in (load, start, mass))
     dma = pltpu.SemaphoreType.DMA
     own, fine = sds(N, N, L), sds(ROWS, COLS, L)
@@ -607,13 +595,11 @@
     rhand = lax.ppermute(hand, "lane", pairs + [(j, i) for i, j in pairs])
     racross = swap_even(rhand, "lane")
 
+    *raw, mass_in = lax.optimization_barrier((*raw, mass_in))
+    load_in, start_in = (pltpu.with_memory_space_constraint(x, pltpu.VMEM) for x in raw)
     u, f, w, a4, v1, v2, v3, cl, token = call(
-        prepare,
-        [fine] * 7 + [own_coarse, sds(8, L)],
-        [HBM, HBM, VM],
-        [own_buf, own_buf, line, dma((2,))],
-        flops=10**8,
-    )(load, start, mass_in)
+        prepare, [fine] * 7 + [own_coarse, sds(8, L)], [VM] * 3, [line], flops=10**8
+    )(load_in, start_in, mass_in)
 
     ce, co = call(pack_corners, [corner, corner], [VM] * 3)(re, ro, token)
     rco, rce = swap_odd(co, "band"), swap_even(ce, "band")

time: 72.4 us -> 72.4 us (level)
  starting transfers between devices: 37.8 us -> 43.7 us
  waiting for transfers between devices: 18.4 us -> 14.2 us
  Pallas kernels: 16 us -> 14.2 us
    ppermute x7, waiting for transfers between devices: 12.1 us -> 7.98 us  [swap_odd(): lax.ppermute(x, axis, [(i, (i + 1) % n if i % 2 else (i - 1) % n) for i i...]
    ppermute x9, starting transfers between devices: 14.2 us -> 18.3 us  [swap_even(): return lax.ppermute(x, axis, [(i, i ^ 1) for i in range(n)])]
    pallas_call x1, Pallas kernels: 6.13 us -> 4.25 us  [shards(): call(prepare, [fine] * 7 + [own_coarse, sds(8, L)], [VM] * 3, [line], flo...]
    ppermute x7, starting transfers between devices: 22.2 us -> 24 us  [swap_odd(): lax.ppermute(x, axis, [(i, (i + 1) % n if i % 2 else (i - 1) % n) for i i...]
  transfers between devices with their start and end apart: 18 -> 18, of which waited for: 4 -> 4; matrix products, arithmetic and copies ran while one was open for 0% -> 0% of each run, Pallas kernels for 12% -> 10%
where the time goes in v4:
time: 72.4 us; the launch traced here: 72.3 us
  starting transfers between devices  43.7 us (60%)
  Pallas kernels  14.2 us (20%)
  waiting for transfers between devices  14.2 us (20%)
    ppermute x7, starting transfers between devices, swap_odd(): lax.ppermute(x, axis, [(i, (i + 1) % n if i % 2 else (i - 1) % n) for i i...  24 us
    ppermute x9, starting transfers between devices, swap_even(): return lax.ppermute(x, axis, [(i, i ^ 1) for i in range(n)])  18.3 us
    ppermute x7, waiting for transfers between devices, swap_odd(): lax.ppermute(x, axis, [(i, (i + 1) % n if i % 2 else (i - 1) % n) for i i...  7.98 us
    ppermute x9, waiting for transfers between devices, swap_even(): return lax.ppermute(x, axis, [(i, i ^ 1) for i in range(n)])  6.2 us
    pallas_call x1, Pallas kernels, shards(): call(after, [own, coarse, coarse], [VM] * 8, [coarse_buf] + [pltpu.VMEM((...  4.67 us
    pallas_call x1, Pallas kernels, shards(): call(prepare, [fine] * 7 + [own_coarse, sds(8, L)], [VM] * 3, [line], flo...  4.25 us
    pallas_call x1, Pallas kernels, shards(): call(pack_fine, [lane_msg, lane_msg, band_msg, band_msg, own, own_coarse,...  2.6 us
  transfers between devices with their start and end apart: 18, of which 4 were waited for; matrix products, arithmetic and copies ran while one was open for 0% of the time, Pallas kernels for 10%

profile of v4, /device:TPU:1, one launch (start us, length us, event | category | flops | bytes accessed | tf_op | source)
XLA Modules:
  0.0 72.3 jit_solution(720016480920216439)
XLA Ops:
  0.0 0.0 copy-start
  0.0 0.0 copy-start.1
  0.0 2.6 %shard_map.37 = (f32[640,128]{1,0:T(8,128)S(1)}, f32[640,128]{1,0:T(8,128)S(1)}, f32[10,64,128]{2,1,0:T(8,128)S(1)}, f32[10,64,128]{2,1,0:T(8,128)S(1)}, f32[64,...) custom-call(f32[64,64,128]{2,1,0:T(8,128)} %load.2, ...), custom_call_target="tpu_custom_call" | custom-call | flops 1000000 | bytes 8000000 | tf_op jit(solution)/shard_map/pallas_call | solution.py:579
  2.6 2.1 %collective-permute-start = (f32[640,128]{1,0:T(8,128)S(1)}, f32[640,128]{1,0:T(8,128)S(1)}, u32[]{:S(2)}, u32[]{:S(2)}) collective-permute-start(f32[640,128]{1,0:T(8,128)S(1)} %get-tuple-element.65), channel_id=1, source_target_pairs={{0,1},{1,0},{2,3},{3,2},{4,5},{5,4},{6,7},{7,6},{8,9},{9,8},{10,11... | collective-permute-start | bytes 983048 | tf_op jit(solution)/shard_map/ppermute | solution.py:557
  4.7 10.9 %collective-permute-start.1 = (f32[640,128]{1,0:T(8,128)S(1)}, f32[640,128]{1,0:T(8,128)S(1)}, u32[]{:S(2)}, u32[]{:S(2)}) collective-permute-start(f32[640,128]{1,0:T(8,128)S(1)} %get-tuple-element.66), channel_id=1, source_target_pairs={{0,31},{1,2},{2,1},{3,4},{4,3},{5,6},{6,5},{7,8},{8,7},{9,10},{10,... | collective-permute-start | bytes 983048 | tf_op jit(solution)/shard_map/ppermute | solution.py:562
  15.6 1.2 %collective-permute-start.2 = (f32[10,64,128]{2,1,0:T(8,128)S(1)}, f32[10,64,128]{2,1,0:T(8,128)S(1)}, u32[]{:S(2)}, u32[]{:S(2)}) collective-permute-start(f32[10,64,128]{2,1,0:T(8,128)S(1)} %get-tuple-element.74), channel_id=1, source_target_pairs={{0,32},{32,0},{64,96},{96,64},{128,160},{160,128},{192,224},{224,1... | collective-permute-start | bytes 983048 | tf_op jit(solution)/shard_map/ppermute | solution.py:557
  16.9 0.0 collective-permute-start.8
  16.9 0.6 collective-permute-start.3
  17.5 6.2 %collective-permute-done.8.edges = f32[416,128]{1,0:T(8,128)S(1)} collective-permute-done((f32[416,128]{1,0:T(8,128)S(1)}, f32[416,128]{1,0:T(8,128)S(1)}, u32[]{:S(2)}, u32[]{:S(2)}) %collective-permute-start.8) | collective-permute-done | bytes 213024 | tf_op jit(solution)/shard_map/ppermute | solution.py:557
  23.7 0.7 collective-permute-start.10
  24.4 0.0 copy-done
  24.4 0.0 copy-done.1
  24.4 4.3 %shard_map.38 = (f32[72,88,128]{2,1,0:T(8,128)S(1)}, f32[72,88,128]{2,1,0:T(8,128)S(1)}, f32[72,88,128]{2,1,0:T(8,128)S(1)}, f32[72,88,128]{2,1,0:T(8,128)S(1)},...) custom-call(f32[64,64,128]{2,1,0:T(8,128)S(1)} %copy-done, ...), custom_call_target="tpu_custom_call" | custom-call | flops 100000000 | bytes 8000000 | tf_op jit(solution)/shard_map/pallas_call | solution.py:600
  28.6 0.0 collective-permute-done.re.m_even
  28.6 0.0 collective-permute-done.1.ro.m_odd
  28.7 3.3 %collective-permute-start.4 = (f32[60,128]{1,0:T(8,128)S(1)}, f32[60,128]{1,0:T(8,128)S(1)}, u32[]{:S(2)}, u32[]{:S(2)}) collective-permute-start(f32[60,128]{1,0:T(8,128)S(1)} %get-tuple-element.77), channel_id=1, source_target_pairs={{0,32},{32,0},{64,96},{96,64},{128,160},{160,128},{192,224},{224,1... | collective-permute-start | bytes 92168 | tf_op jit(solution)/shard_map/ppermute | solution.py:557
  32.0 1.8 %collective-permute-start.5 = (f32[60,128]{1,0:T(8,128)S(1)}, f32[60,128]{1,0:T(8,128)S(1)}, u32[]{:S(2)}, u32[]{:S(2)}) collective-permute-start(f32[60,128]{1,0:T(8,128)S(1)} %get-tuple-element.78), channel_id=1, source_target_pairs={{0,224},{32,64},{64,32},{96,128},{128,96},{160,192},{192,160},{224... | collective-permute-start | bytes 92168 | tf_op jit(solution)/shard_map/ppermute | solution.py:562
  33.8 0.0 collective-permute-done.10
  33.8 0.7 collective-permute-start.9
  34.4 0.0 collective-permute-done.2.be
  34.4 6.5 %collective-permute-start.11 = (f32[208,128]{1,0:T(8,128)S(1)}, f32[208,128]{1,0:T(8,128)S(1)}, u32[]{:S(2)}, u32[]{:S(2)}) collective-permute-start(f32[208,128]{1,0:T(8,128)S(1)} %collective-permute-done.10), channel_id=1, source_target_pairs={{0,1},{1,0},{2,3},{3,2},{4,5},{5,4},{6,7},{7,6},{8,9},{9,8},{10,11... | collective-permute-start | bytes 319496 | tf_op jit(solution)/shard_map/ppermute | solution.py:557
  40.9 1.3 %shard_map.39 = (f32[72,88,128]{2,1,0:T(8,128)S(1)}, f32[72,88,128]{2,1,0:T(8,128)S(1)}, f32[72,88,128]{2,1,0:T(8,128)S(1)}, f32[72,88,128]{2,1,0:T(8,128)S(1)},...) custom-call(f32[72,88,128]{2,1,0:T(8,128)S(1)} %get-tuple-element.57, ...), custom_call_target="tpu_custom_call", output_to_operand_aliasing={{0}: (0, {}), {1}: (1, {}), {2}: (2, {}), {3}: (3, {}), {4}... | custom-call | flops 10000000 | bytes 8000000 | tf_op jit(solution)/shard_map/pallas_call | solution.py:612
  42.2 0.0 collective-permute-done.3.bo
  42.2 0.0 collective-permute-done.4.ce
  42.3 0.0 collective-permute-done.5.co
  42.3 0.6 shard_map.41
  42.9 0.1 collective-permute-start.6
  43.0 1.2 %collective-permute-start.14 = (f32[280,128]{1,0:T(8,128)S(1)}, f32[280,128]{1,0:T(8,128)S(1)}, u32[]{:S(2)}, u32[]{:S(2)}) collective-permute-start(f32[280,128]{1,0:T(8,128)S(1)} %get-tuple-element.90), channel_id=1, source_target_pairs={{0,32},{32,0},{64,96},{96,64},{128,160},{160,128},{192,224},{224,1... | collective-permute-start | bytes 430088 | tf_op jit(solution)/shard_map/ppermute | solution.py:557
  44.2 5.7 %collective-permute-start.7 = (f32[272,128]{1,0:T(8,128)S(1)}, f32[272,128]{1,0:T(8,128)S(1)}, u32[]{:S(2)}, u32[]{:S(2)}) collective-permute-start(f32[272,128]{1,0:T(8,128)S(1)} %get-tuple-element.82), channel_id=1, source_target_pairs={{0,31},{1,2},{2,1},{3,4},{4,3},{5,6},{6,5},{7,8},{8,7},{9,10},{10,... | collective-permute-start | bytes 417800 | tf_op jit(solution)/shard_map/ppermute | solution.py:562
  49.9 0.0 collective-permute-done.9.near
  49.9 0.0 collective-permute-done.11.across
  49.9 0.1 shard_map.44
  50.0 0.5 collective-permute-start.12
  50.4 1.4 %collective-permute-start.13 = (f32[392,128]{1,0:T(8,128)S(1)}, f32[392,128]{1,0:T(8,128)S(1)}, u32[]{:S(2)}, u32[]{:S(2)}) collective-permute-start(f32[392,128]{1,0:T(8,128)S(1)} %get-tuple-element.89), channel_id=1, source_target_pairs={{0,224},{32,64},{64,32},{96,128},{128,96},{160,192},{192,160},{224... | collective-permute-start | bytes 602120 | tf_op jit(solution)/shard_map/ppermute | solution.py:562
  51.9 0.0 collective-permute-done.6.re.le
  51.9 0.3 collective-permute-start.15
  52.2 5.4 %collective-permute-done.7.ro.lo = f32[272,128]{1,0:T(8,128)S(1)} collective-permute-done((f32[272,128]{1,0:T(8,128)S(1)}, f32[272,128]{1,0:T(8,128)S(1)}, u32[]{:S(2)}, u32[]{:S(2)}) %collective-permute-start.7) | collective-permute-done | bytes 139296 | tf_op jit(solution)/shard_map/ppermute | solution.py:562
  57.6 0.1 shard_map.42
  57.6 3.5 %collective-permute-start.16 = (f32[184,128]{1,0:T(8,128)S(1)}, f32[184,128]{1,0:T(8,128)S(1)}, u32[]{:S(2)}, u32[]{:S(2)}) collective-permute-start(f32[184,128]{1,0:T(8,128)S(1)} %get-tuple-element.98), channel_id=1, source_target_pairs={{0,32},{32,0},{64,96},{96,64},{128,160},{160,128},{192,224},{224,1... | collective-permute-start | bytes 282632 | tf_op jit(solution)/shard_map/ppermute | solution.py:557
  61.1 0.0 collective-permute-done.14.rbe
  61.1 3.3 %collective-permute-start.17 = (f32[184,128]{1,0:T(8,128)S(1)}, f32[184,128]{1,0:T(8,128)S(1)}, u32[]{:S(2)}, u32[]{:S(2)}) collective-permute-start(f32[184,128]{1,0:T(8,128)S(1)} %get-tuple-element.99), channel_id=1, source_target_pairs={{0,224},{32,64},{64,32},{96,128},{128,96},{160,192},{192,160},{224... | collective-permute-start | bytes 282632 | tf_op jit(solution)/shard_map/ppermute | solution.py:562
  64.4 2.0 %collective-permute-done.15.rbo = f32[280,128]{1,0:T(8,128)S(1)} collective-permute-done((f32[280,128]{1,0:T(8,128)S(1)}, f32[280,128]{1,0:T(8,128)S(1)}, u32[]{:S(2)}, u32[]{:S(2)}) %collective-permute-start.15) | collective-permute-done | bytes 143392 | tf_op jit(solution)/shard_map/ppermute | solution.py:562
  66.4 0.0 collective-permute-done.12.mbe
  66.4 0.0 collective-permute-done.13.mbo
  66.4 0.6 shard_map.45
  67.0 0.0 collective-permute-done.16.lbe
  67.0 0.6 collective-permute-done.17.lbo
  67.6 4.7 %shard_map.46 = (f32[64,64,128]{2,1,0:T(8,128)}, f32[42,56,128]{2,1,0:T(8,128)S(1)}, f32[42,56,128]{2,1,0:T(8,128)S(1)}) custom-call(f32[72,88,128]{2,1,0:T(8,128)S(1)} %get-tuple-element.92.v, f32[72,88,128]{2,1,0:T(8,128)S(1)} %get-tuple-element.93.f, f32[72,88,128]{2,1,0:T(8,128)S(1)} %get-tuple-element.94.w, ...), custom_call_target="tpu_custom_call", output_to_operand_aliasing={{1}: (4, {}), {2}: (5, {})} | custom-call | flops 100000000 | bytes 8000000 | tf_op jit(solution)/shard_map/pallas_call | solution.py:642
  (2 shorter events, 0.0 us)
Async XLA Ops:
  0.0 24.4 %copy-start = (f32[64,64,128]{2,1,0:T(8,128)S(1)}, f32[64,64,128]{2,1,0:T(8,128)}, u32[]{:S(2)}) copy-start(f32[64,64,128]{2,1,0:T(8,128)} %load.2) | copy-start | bytes 6291460
  0.0 24.4 %copy-start.1 = (f32[64,64,128]{2,1,0:T(8,128)S(1)}, f32[64,64,128]{2,1,0:T(8,128)}, u32[]{:S(2)}) copy-start(f32[64,64,128]{2,1,0:T(8,128)} %start.2) | copy-start | bytes 6291460
  2.6 26.0 %collective-permute-start = (f32[640,128]{1,0:T(8,128)S(1)}, f32[640,128]{1,0:T(8,128)S(1)}, u32[]{:S(2)}, u32[]{:S(2)}) collective-permute-start(f32[640,128]{1,0:T(8,128)S(1)} %get-tuple-element.65), channel_id=1, source_target_pairs={{0,1},{1,0},{2,3},{3,2},{4,5},{5,4},{6,7},{7,6},{8,9},{9,8},{10,11... | collective-permute-start | bytes 983048 | tf_op jit(solution)/shard_map/ppermute | solution.py:557
  4.7 23.9 %collective-permute-start.1 = (f32[640,128]{1,0:T(8,128)S(1)}, f32[640,128]{1,0:T(8,128)S(1)}, u32[]{:S(2)}, u32[]{:S(2)}) collective-permute-start(f32[640,128]{1,0:T(8,128)S(1)} %get-tuple-element.66), channel_id=1, source_target_pairs={{0,31},{1,2},{2,1},{3,4},{4,3},{5,6},{6,5},{7,8},{8,7},{9,10},{10,... | collective-permute-start | bytes 983048 | tf_op jit(solution)/shard_map/ppermute | solution.py:562
  15.6 18.8 %collective-permute-start.2 = (f32[10,64,128]{2,1,0:T(8,128)S(1)}, f32[10,64,128]{2,1,0:T(8,128)S(1)}, u32[]{:S(2)}, u32[]{:S(2)}) collective-permute-start(f32[10,64,128]{2,1,0:T(8,128)S(1)} %get-tuple-element.74), channel_id=1, source_target_pairs={{0,32},{32,0},{64,96},{96,64},{128,160},{160,128},{192,224},{224,1... | collective-permute-start | bytes 983048 | tf_op jit(solution)/shard_map/ppermute | solution.py:557
  16.9 6.8 %collective-permute-start.8 = (f32[416,128]{1,0:T(8,128)S(1)}, f32[416,128]{1,0:T(8,128)S(1)}, u32[]{:S(2)}, u32[]{:S(2)}) collective-permute-start(f32[416,128]{1,0:T(8,128)S(1)} %get-tuple-element.85), channel_id=1, source_target_pairs={{0,1},{1,0},{2,3},{3,2},{4,5},{5,4},{6,7},{7,6},{8,9},{9,8},{10,11... | collective-permute-start | bytes 638984 | tf_op jit(solution)/shard_map/ppermute | solution.py:557
  16.9 25.4 %collective-permute-start.3 = (f32[10,64,128]{2,1,0:T(8,128)S(1)}, f32[10,64,128]{2,1,0:T(8,128)S(1)}, u32[]{:S(2)}, u32[]{:S(2)}) collective-permute-start(f32[10,64,128]{2,1,0:T(8,128)S(1)} %get-tuple-element.75), channel_id=1, source_target_pairs={{0,224},{32,64},{64,32},{96,128},{128,96},{160,192},{192,160},{224... | collective-permute-start | bytes 983048 | tf_op jit(solution)/shard_map/ppermute | solution.py:562
  23.7 10.1 %collective-permute-start.10 = (f32[208,128]{1,0:T(8,128)S(1)}, f32[208,128]{1,0:T(8,128)S(1)}, u32[]{:S(2)}, u32[]{:S(2)}) collective-permute-start(f32[208,128]{1,0:T(8,128)S(1)} %shard_map.43), channel_id=1, source_target_pairs={{14,17},{30,1},{17,14},{1,30},{46,49},{62,33},{49,46},{33,62},{78,... | collective-permute-start | bytes 319496 | tf_op jit(solution)/shard_map/ppermute | solution.py:595
  28.7 13.6 %collective-permute-start.4 = (f32[60,128]{1,0:T(8,128)S(1)}, f32[60,128]{1,0:T(8,128)S(1)}, u32[]{:S(2)}, u32[]{:S(2)}) collective-permute-start(f32[60,128]{1,0:T(8,128)S(1)} %get-tuple-element.77), channel_id=1, source_target_pairs={{0,32},{32,0},{64,96},{96,64},{128,160},{160,128},{192,224},{224,1... | collective-permute-start | bytes 92168 | tf_op jit(solution)/shard_map/ppermute | solution.py:557
  32.0 10.3 %collective-permute-start.5 = (f32[60,128]{1,0:T(8,128)S(1)}, f32[60,128]{1,0:T(8,128)S(1)}, u32[]{:S(2)}, u32[]{:S(2)}) collective-permute-start(f32[60,128]{1,0:T(8,128)S(1)} %get-tuple-element.78), channel_id=1, source_target_pairs={{0,224},{32,64},{64,32},{96,128},{128,96},{160,192},{192,160},{224... | collective-permute-start | bytes 92168 | tf_op jit(solution)/shard_map/ppermute | solution.py:562
  33.8 16.1 %collective-permute-start.9 = (f32[208,128]{1,0:T(8,128)S(1)}, f32[208,128]{1,0:T(8,128)S(1)}, u32[]{:S(2)}, u32[]{:S(2)}) collective-permute-start(f32[208,128]{1,0:T(8,128)S(1)} %get-tuple-element.86), channel_id=1, source_target_pairs={{1,2},{3,4},{5,6},{7,8},{9,10},{11,12},{13,14},{17,18},{19,20},{21... | collective-permute-start | bytes 319496 | tf_op jit(solution)/shard_map/ppermute | solution.py:592
  34.4 15.4 %collective-permute-start.11 = (f32[208,128]{1,0:T(8,128)S(1)}, f32[208,128]{1,0:T(8,128)S(1)}, u32[]{:S(2)}, u32[]{:S(2)}) collective-permute-start(f32[208,128]{1,0:T(8,128)S(1)} %collective-permute-done.10), channel_id=1, source_target_pairs={{0,1},{1,0},{2,3},{3,2},{4,5},{5,4},{6,7},{7,6},{8,9},{9,8},{10,11... | collective-permute-start | bytes 319496 | tf_op jit(solution)/shard_map/ppermute | solution.py:557
  42.9 9.0 %collective-permute-start.6 = (f32[272,128]{1,0:T(8,128)S(1)}, f32[272,128]{1,0:T(8,128)S(1)}, u32[]{:S(2)}, u32[]{:S(2)}) collective-permute-start(f32[272,128]{1,0:T(8,128)S(1)} %get-tuple-element.81), channel_id=1, source_target_pairs={{0,1},{1,0},{2,3},{3,2},{4,5},{5,4},{6,7},{7,6},{8,9},{9,8},{10,11... | collective-permute-start | bytes 417800 | tf_op jit(solution)/shard_map/ppermute | solution.py:557
  43.0 18.1 %collective-permute-start.14 = (f32[280,128]{1,0:T(8,128)S(1)}, f32[280,128]{1,0:T(8,128)S(1)}, u32[]{:S(2)}, u32[]{:S(2)}) collective-permute-start(f32[280,128]{1,0:T(8,128)S(1)} %get-tuple-element.90), channel_id=1, source_target_pairs={{0,32},{32,0},{64,96},{96,64},{128,160},{160,128},{192,224},{224,1... | collective-permute-start | bytes 430088 | tf_op jit(solution)/shard_map/ppermute | solution.py:557
  44.2 13.4 %collective-permute-start.7 = (f32[272,128]{1,0:T(8,128)S(1)}, f32[272,128]{1,0:T(8,128)S(1)}, u32[]{:S(2)}, u32[]{:S(2)}) collective-permute-start(f32[272,128]{1,0:T(8,128)S(1)} %get-tuple-element.82), channel_id=1, source_target_pairs={{0,31},{1,2},{2,1},{3,4},{4,3},{5,6},{6,5},{7,8},{8,7},{9,10},{10,... | collective-permute-start | bytes 417800 | tf_op jit(solution)/shard_map/ppermute | solution.py:562
  50.0 16.5 %collective-permute-start.12 = (f32[392,128]{1,0:T(8,128)S(1)}, f32[392,128]{1,0:T(8,128)S(1)}, u32[]{:S(2)}, u32[]{:S(2)}) collective-permute-start(f32[392,128]{1,0:T(8,128)S(1)} %get-tuple-element.88), channel_id=1, source_target_pairs={{0,32},{32,0},{64,96},{96,64},{128,160},{160,128},{192,224},{224,1... | collective-permute-start | bytes 602120 | tf_op jit(solution)/shard_map/ppermute | solution.py:557
  50.4 16.0 %collective-permute-start.13 = (f32[392,128]{1,0:T(8,128)S(1)}, f32[392,128]{1,0:T(8,128)S(1)}, u32[]{:S(2)}, u32[]{:S(2)}) collective-permute-start(f32[392,128]{1,0:T(8,128)S(1)} %get-tuple-element.89), channel_id=1, source_target_pairs={{0,224},{32,64},{64,32},{96,128},{128,96},{160,192},{192,160},{224... | collective-permute-start | bytes 602120 | tf_op jit(solution)/shard_map/ppermute | solution.py:562
  51.9 14.5 %collective-permute-start.15 = (f32[280,128]{1,0:T(8,128)S(1)}, f32[280,128]{1,0:T(8,128)S(1)}, u32[]{:S(2)}, u32[]{:S(2)}) collective-permute-start(f32[280,128]{1,0:T(8,128)S(1)} %get-tuple-element.91), channel_id=1, source_target_pairs={{0,224},{32,64},{64,32},{96,128},{128,96},{160,192},{192,160},{224... | collective-permute-start | bytes 430088 | tf_op jit(solution)/shard_map/ppermute | solution.py:562
  57.6 9.4 %collective-permute-start.16 = (f32[184,128]{1,0:T(8,128)S(1)}, f32[184,128]{1,0:T(8,128)S(1)}, u32[]{:S(2)}, u32[]{:S(2)}) collective-permute-start(f32[184,128]{1,0:T(8,128)S(1)} %get-tuple-element.98), channel_id=1, source_target_pairs={{0,32},{32,0},{64,96},{96,64},{128,160},{160,128},{192,224},{224,1... | collective-permute-start | bytes 282632 | tf_op jit(solution)/shard_map/ppermute | solution.py:557
  61.1 6.5 %collective-permute-start.17 = (f32[184,128]{1,0:T(8,128)S(1)}, f32[184,128]{1,0:T(8,128)S(1)}, u32[]{:S(2)}, u32[]{:S(2)}) collective-permute-start(f32[184,128]{1,0:T(8,128)S(1)} %get-tuple-element.99), channel_id=1, source_target_pairs={{0,224},{32,64},{64,32},{96,128},{128,96},{160,192},{192,160},{224... | collective-permute-start | bytes 282632 | tf_op jit(solution)/shard_map/ppermute | solution.py:562
